TPU v7x, 512 devices: a whole 4x8x8 slice. The times are simulated.
512 devices in a mesh: dp: 64 (over y, z), tensor: 8 (over x, core).
Axes of the slice: x: 4, y: 8, z: 8, core: 2. Of those that a mesh axis runs over, the one named last changes fastest.
Arguments:
- streams: bfloat16 [8192, 4, 8192], P('dp', None, 'tensor'), may hold values from -6 to 6
- layer_out: bfloat16 [8192, 8192], P('dp', 'tensor'), may hold values from -6 to 6
- cotangent: bfloat16 [8192, 4, 8192], P('dp', None, 'tensor'), may hold values from -6 to 6
- input_cot: bfloat16 [8192, 8192], P('dp', 'tensor'), may hold values from -6 to 6
- gain: float32 [8192], P('tensor'), may hold values from 0.5 to 1.5
- projection: float32 [6, 8192], P(None, 'tensor'), may hold values from -0.0625 to 0.0625
- static_mix: float32 [4, 6], replicated, may hold values from -3 to 3
- tanh_scale: float32 [3], replicated, may hold values from 0.5 to 2
Outputs:
- stream_grad: bfloat16 [8192, 4, 8192], P('dp', None, 'tensor')
- out_grad: bfloat16 [8192, 8192], P('dp', 'tensor')
- proj_grad: float32 [6, 8192], P(None, 'tensor')
- gain_grad: float32 [8192], P('tensor')
All inputs are finite; a program needn't handle non-finite values.
Results may differ from a plain program's by a relative error of at most 0.0018.
Values sent between devices are 32-bit elements; how exact they have to be, the bound alone decides.
A program may use at most 64 MiB of HBM per device.

v0:
```python
import jax
import jax.numpy as jnp
from jax import lax
from jax.sharding import PartitionSpec as P

D = 8192


def sent_to_all(x, axis):
    size = lax.axis_size(axis)
    return lax.all_to_all(jnp.broadcast_to(x[None], (size, *x.shape)), axis, 0, 0, tiled=True)


def over_copies(x, axis):
    return sent_to_all(x, axis).sum(axis=0)


def together(arrays, axis):
    vector, at, outs = (jnp.concatenate([a.reshape(-1) for a in arrays]), 0, [])
    so_far = over_copies(vector, axis)
    for a in arrays:
        outs.append(so_far[at : at + a.size].reshape(a.shape))
        at += a.size
    return tuple(outs)


def nonlinear(square, lin, dbeta, dalpha, dmixer, static_mix, tanh_scale):
    inv_rms = lax.rsqrt(square / D + 1e-06)
    bent = jnp.tanh(inv_rms[..., None] * lin)
    scales = jnp.concatenate([tanh_scale[0:2], jnp.repeat(tanh_scale[2:3], 4)])
    coef = static_mix[None] + scales * bent
    dcoef = jnp.concatenate([dbeta[..., None], dalpha[..., None], dmixer], axis=-1)
    dpre = dcoef * scales * (1.0 - bent * bent)
    dlin = dpre * inv_rms[..., None]
    dsquare = -0.5 * inv_rms**3 / D * jnp.sum(dpre * lin, axis=-1)
    return (coef, dlin, dsquare)


def shards(streams, layer_out, cotangent, input_cot, gain, projection, static_mix, tanh_scale):
    wproj = gain[None, :] * projection
    square = jnp.einsum("tjd,tjd->tj", streams, streams, preferred_element_type=jnp.float32)
    lin = jnp.stack([jnp.sum(streams * wproj[column], axis=-1) for column in range(6)], axis=-1)
    dbeta = jnp.einsum("td,tkd->tk", layer_out, cotangent, preferred_element_type=jnp.float32)
    dalpha = jnp.einsum("tjd,td->tj", streams, input_cot, preferred_element_type=jnp.float32)
    dmixer = jnp.einsum("tjd,tkd->tjk", streams, cotangent, preferred_element_type=jnp.float32)
    square, lin, dbeta, dalpha, dmixer = together((square, lin, dbeta, dalpha, dmixer), "tensor")
    coef, dlin, dsquare = nonlinear(square, lin, dbeta, dalpha, dmixer, static_mix, tanh_scale)
    out_total = coef[:, 0, 0][:, None] * cotangent[:, 0, :]
    for stream in range(1, 4):
        out_total = out_total + coef[:, stream, 0][:, None] * cotangent[:, stream, :]
    out_grad = out_total.astype(jnp.bfloat16)
    total = coef[:, :, 1][..., None] * input_cot[:, None, :]
    for stream in range(4):
        total = total + coef[:, :, 2 + stream][..., None] * cotangent[:, stream, :][:, None, :]
    for column in range(6):
        total = total + dlin[:, :, column][..., None] * wproj[column]
    total = total + (2.0 * dsquare)[..., None] * streams
    stream_grad = total.astype(jnp.bfloat16)
    dweight = jnp.stack(
        [jnp.sum(dlin[:, :, column][..., None] * streams, axis=(0, 1)) for column in range(6)],
        axis=0,
    )
    proj_part = gain[None, :] * dweight
    gain_part = jnp.sum(dweight * projection, axis=0)
    proj_sum, gain_sum = together((proj_part, gain_part), "dp")
    all_tokens = streams.shape[0] * lax.axis_size("dp")
    proj_grad = proj_sum / jnp.sqrt(4.0 * all_tokens * D)
    gain_grad = gain_sum / jnp.sqrt(4.0 * all_tokens)
    return (stream_grad, out_grad, proj_grad, gain_grad)


def solution(mesh):
    placed = (
        P("dp", None, "tensor"),
        P("dp", "tensor"),
        P("dp", None, "tensor"),
        P("dp", "tensor"),
        P("tensor"),
        P(None, "tensor"),
        P(),
        P(),
    )
    return jax.shard_map(
        shards,
        mesh=mesh,
        in_specs=placed,
        out_specs=(P("dp", None, "tensor"), P("dp", "tensor"), P(None, "tensor"), P("tensor")),
        check_vma=False,
    )
```

profile of v0, /device:TPU:24, one launch (start us, length us, event | category | flops | bytes accessed | tf_op | source)
XLA Modules:
  0.0 103.4 jit_solution(9548949053168461121)
XLA Ops:
  0.7 0.9 broadcast_multiply_fusion.2
  1.6 4.8 %fusion.6 = (f32[128,4]{1,0:T(8,128)S(1)}, f32[128,4]{1,0:T(8,128)S(1)}, f32[128,4]{1,0:T(8,128)S(1)}, f32[128,4]{1,0:T(8,128)S(1)}, f32[128,4]{1,0:T(8,128)S(1)...) fusion(bf16[128,4,1024]{2,1,0:T(4,128)(2,1)} %param.8, f32[1024]{0:T(1024)S(1)} %bitcast.80, f32[1024]{0:T(1024)S(1)} %bitcast.88, ...), kind=kLoop, calls=%fused_computation.20 | loop fusion | flops 7860736 | bytes 1087488 | tf_op jit(solution)/shard_map/reduce_sum | solution.py:42
  6.9 0.2 copy.219
  7.1 0.3 reshape.122
  7.5 1.1 %fusion.35 = f32[128,4,4]{2,1,0:T(4,128)S(1)} fusion(bf16[128,4,1024]{2,1,0:T(4,128)(2,1)S(1)} %copy-done, bf16[128,4,1024]{2,1,0:T(4,128)(2,1)S(1)} %copy-done.5), kind=kOutput, calls=%fused_computation.81 | convolution fusion | flops 4194304 | bytes 2105344 | tf_op jit(solution)/shard_map/tjd,tkd->tjk/dot_general | solution.py:45
  8.7 1.2 %fusion.17 = f32[128,1,4]{2,1,0:T(1,128)S(1)} fusion(bf16[128,4,1024]{2,1,0:T(4,128)(2,1)S(1)} %copy-done.5, bf16[128,1024,1]{1,0,2:T(8,128)(2,1)S(1)} %bitcast.107), kind=kOutput, calls=%fused_computation.32 | convolution fusion | flops 1048576 | bytes 1312768 | tf_op jit(solution)/shard_map/td,tkd->tk/dot_general | solution.py:43
  10.0 1.1 %fusion.15 = f32[128,1,4]{2,1,0:T(1,128)S(1)} fusion(bf16[128,4,1024]{2,1,0:T(4,128)(2,1)S(1)} %copy-done, bf16[128,1024,1]{1,0,2:T(8,128)(2,1)S(1)} %bitcast.75), kind=kOutput, calls=%fused_computation.30 | convolution fusion | flops 1048576 | bytes 1312768 | tf_op jit(solution)/shard_map/tjd,td->tj/dot_general | solution.py:44
  11.3 0.3 reshape.125
  11.6 0.8 broadcast_in_dim.4
  12.4 4.3 %all-to-all-start = ((f32[8,1,6656]{2,1,0:T(1,128)}), f32[8,1,6656]{2,1,0:T(1,128)S(1)}, u32[]{:S(2)}, u32[]{:S(2)}) async-start(f32[8,1,6656]{2,1,0:T(1,128)} %broadcast_in_dim.4), calls=%async_computation | async-start | bytes 425984 | tf_op jit(solution)/shard_map/all_to_all | solution.py:11
  16.7 0.6 slice.165
  17.3 0.6 concatenate.12
  17.9 5.7 %all-to-all-done = f32[8,1,6656]{2,1,0:T(1,128)S(1)} async-done(((f32[8,1,6656]{2,1,0:T(1,128)}), f32[8,1,6656]{2,1,0:T(1,128)S(1)}, u32[]{:S(2)}, u32[]{:S(2)}) %all-to-all-start) | async-done | bytes 213024 | tf_op jit(solution)/shard_map/all_to_all | solution.py:11
  23.9 0.3 reshape.126
  24.2 0.3 reshape.127
  24.5 0.3 slice.201
  24.9 0.3 slice.202
  25.3 1.2 %broadcast_multiply_fusion = (f32[128,4,6]{2,1,0:T(4,128)S(1)}, f32[128,4,6]{2,1,0:T(4,128)}, f32[128,4,6]{2,1,0:T(4,128)S(1)}) fusion(f32[128,4]{1,0:T(8,128)S(1)} %rsqrt.7, f32[128,4,6]{2,1,0:T(4,128)S(1)} %reshape.126, f32[6]{0:T(128)S(1)} %concatenate.12, f32[128,4,4]{2,1,0:T(4,128)S(1)} %reshape.127, f32[128,4,1]{2,1,0:T(4,128)S(1)} %slice.202, ...), kind=kLoop, calls=%fused_computation.47 | loop fusion | flops 30720 | bytes 63608 | tf_op jit(solution)/shard_map/mul | solution.py:34
  26.5 2.5 %fusion.31 = (f32[128,4,1]{2,1,0:T(4,128)}, f32[128,4,1]{2,1,0:T(4,128)}, f32[128,4,1]{2,1,0:T(4,128)}, f32[128,4,1]{2,1,0:T(4,128)}, f32[128,4,1]{2,1,0:T(4,128...) fusion(f32[128,4,6]{2,1,0:T(4,128)S(1)} %get-tuple-element.27, ...), kind=kLoop, calls=%fused_computation.77 | loop fusion | bytes 45056 | tf_op jit(solution)/shard_map/slice | solution.py:52
  30.5 3.2 %fusion.14 = (f32[1024]{0:T(1024)S(1)}, f32[1024]{0:T(1024)S(1)}, f32[1024]{0:T(1024)S(1)}, f32[1024]{0:T(1024)S(1)}, f32[1024]{0:T(1024)S(1)}, /*index=5*/f32[1024]{0:T(1024)S(1)}) fusion(bf16[128,4,1024]{2,1,0:T(4,128)(2,1)S(1)} %copy-done, f32[128,4]{1,0:T(8,128)S(1)} %copy.248, f32[128,4]{1,0:T(8,128)S(1)} %copy.238, f32[128,4]{1,0:T(8,128)S(1)} %copy.240, ...), kind=kLoop, calls=%fused_computation.28 | loop fusion | flops 6809600 | bytes 1085440 | tf_op jit(solution)/shard_map/reduce_sum | solution.py:60
  33.8 2.2 %broadcast_in_dim.5 = f32[64,1,7168]{2,1,0:T(1,128)} broadcast(f32[7168]{0:T(1024)S(1)} %pad_maximum_fusion), dimensions={2} | broadcast | bytes 1863680 | tf_op jit(solution)/shard_map/broadcast_in_dim | solution.py:11
  36.0 16.4 %all-to-all-start.1 = ((f32[64,1,7168]{2,1,0:T(1,128)}), f32[64,1,7168]{2,1,0:T(1,128)S(1)}, u32[]{:S(2)}, u32[]{:S(2)}) async-start(f32[64,1,7168]{2,1,0:T(1,128)} %broadcast_in_dim.5), calls=%async_computation.1 | async-start | bytes 3670016 | tf_op jit(solution)/shard_map/all_to_all | solution.py:11
  52.5 1.8 %convert_element_type.14 = f32[128,1024]{1,0:T(8,128)} convert(bf16[128,1024]{1,0:T(8,128)(2,1)} %param.11) | non-fusion elementwise | flops 131072 | bytes 786432 | tf_op jit(solution)/shard_map/convert_element_type | solution.py:52
  54.3 4.4 %fusion.30 = (bf16[128,1,1024]{2,1,0:T(2,128)(2,1)S(1)}, bf16[128,1,1024]{2,1,0:T(2,128)(2,1)S(1)}, bf16[128,1,1024]{2,1,0:T(2,128)(2,1)S(1)}, bf16[128,1,1024]{2,1,0:T(2,128)(2,1)S(1)}) fusion(bf16[128,4,1024]{2,1,0:T(4,128)(2,1)} %param.10), kind=kLoop, calls=%fused_computation.76 | loop fusion | bytes 2097152 | tf_op jit(solution)/shard_map/slice | solution.py:54
  58.7 0.8 copy-done.2
  59.4 1.2 %fusion.20 = (f32[128,1024]{1,0:T(8,128)}, f32[128,1024]{1,0:T(8,128)}) fusion(bf16[128,1,1024]{2,1,0:T(2,128)(2,1)S(1)} %get-tuple-element.26, bf16[128,1,1024]{2,1,0:T(2,128)(2,1)S(1)} %get-tuple-element.24), kind=kLoop, calls=%fused_computation.37 | loop fusion | flops 262144 | bytes 1572864 | tf_op jit(solution)/shard_map/mul | solution.py:54
  60.7 1.2 %fusion.22 = (f32[128,1024]{1,0:T(8,128)}, f32[128,1024]{1,0:T(8,128)}) fusion(bf16[128,1,1024]{2,1,0:T(2,128)(2,1)S(1)} %get-tuple-element.25, bf16[128,1,1024]{2,1,0:T(2,128)(2,1)S(1)} %get-tuple-element.23), kind=kLoop, calls=%fused_computation.41 | loop fusion | flops 262144 | bytes 1572864 | tf_op jit(solution)/shard_map/mul | solution.py:54
  61.8 1.5 %copy.249 = f32[128,4]{0,1:T(4,128)} copy(f32[128,4]{1,0:T(8,128)} %copy-done.17) | data formatting | bytes 4096 | tf_op jit(solution)/shard_map/rsqrt | solution.py:28
  63.3 1.6 %copy.221 = f32[128,4,1]{0,1,2:T(4,128)} copy(f32[128,4,1]{2,1,0:T(4,128)} %get-tuple-element.28) | data formatting | bytes 4096 | tf_op jit(solution)/shard_map/slice | solution.py:52
  65.0 1.4 %copy.222 = f32[128,4]{1,0:T(8,128)} copy(f32[128,4]{0,1:T(4,128)} %bitcast.102) | data formatting | bytes 4096 | tf_op jit(solution)/shard_map/mul | solution.py:52
  66.3 1.6 %copy.223 = f32[128,4,1]{0,1,2:T(4,128)} copy(f32[128,4,1]{2,1,0:T(4,128)} %get-tuple-element.32) | data formatting | bytes 4096 | tf_op jit(solution)/shard_map/slice | solution.py:54
  68.0 1.4 %copy.224 = f32[128,4]{1,0:T(8,128)} copy(f32[128,4]{0,1:T(4,128)} %bitcast.103) | data formatting | bytes 4096 | tf_op jit(solution)/shard_map/mul | solution.py:54
  69.4 1.6 %copy.226 = f32[128,4,1]{0,1,2:T(4,128)} copy(f32[128,4,1]{2,1,0:T(4,128)} %get-tuple-element.31) | data formatting | bytes 4096 | tf_op jit(solution)/shard_map/slice | solution.py:54
  71.0 1.4 %copy.227 = f32[128,4]{1,0:T(8,128)} copy(f32[128,4]{0,1:T(4,128)} %bitcast.104) | data formatting | bytes 4096 | tf_op jit(solution)/shard_map/mul | solution.py:54
  72.4 1.6 %copy.229 = f32[128,4,1]{0,1,2:T(4,128)} copy(f32[128,4,1]{2,1,0:T(4,128)} %get-tuple-element.30) | data formatting | bytes 4096 | tf_op jit(solution)/shard_map/slice | solution.py:54
  74.1 1.4 %copy.230 = f32[128,4]{1,0:T(8,128)} copy(f32[128,4]{0,1:T(4,128)} %bitcast.105) | data formatting | bytes 4096 | tf_op jit(solution)/shard_map/mul | solution.py:54
  75.5 1.6 %copy.232 = f32[128,4,1]{0,1,2:T(4,128)} copy(f32[128,4,1]{2,1,0:T(4,128)} %get-tuple-element.29) | data formatting | bytes 4096 | tf_op jit(solution)/shard_map/slice | solution.py:54
  77.1 1.4 %copy.233 = f32[128,4]{1,0:T(8,128)} copy(f32[128,4]{0,1:T(4,128)} %bitcast.106) | data formatting | bytes 4096 | tf_op jit(solution)/shard_map/mul | solution.py:54
  78.5 1.8 %multiply_reduce_fusion = f32[128,4]{1,0:T(8,128)} fusion(f32[128,4,6]{2,1,0:T(4,128)} %get-tuple-element.22, f32[128,4,6]{2,1,0:T(4,128)S(1)} %reshape.126), kind=kLoop, calls=%fused_computation.44 | loop fusion | flops 5632 | bytes 26624 | tf_op jit(solution)/shard_map/reduce_sum | solution.py:35
  80.3 0.9 copy.252
  81.2 0.7 fusion.26
  82.1 1.1 %slice_reduce_fusion.3 = (f32[128]{0:T(128)S(1)}, f32[128]{0:T(128)S(1)}, f32[128]{0:T(128)S(1)}, f32[128]{0:T(128)S(1)}) fusion(f32[128,4,6]{2,1,0:T(4,128)S(1)} %get-tuple-element.27), kind=kLoop, calls=%fused_computation.51 | loop fusion | bytes 4096 | tf_op jit(solution)/shard_map/slice | solution.py:48
  83.2 2.6 %add_convert_fusion = bf16[128,1024]{1,0:T(8,128)(2,1)} fusion(f32[128]{0:T(128)S(1)} %get-tuple-element.18, f32[128]{0:T(128)S(1)} %get-tuple-element.19, f32[128]{0:T(128)S(1)} %get-tuple-element.20, f32[128]{0:T(128)S(1)} %get-tuple-element.17, bf16[128,1,1024]{2,1,0:T(2,128)(2,1)} %copy-done.1, bf16[128,1,1024]{2,1,0:T(2,128)(2,1)} %copy-done.3, ...), kind=kLoop, calls=%fused_computation.29 | loop fusion | flops 1572864 | bytes 1312768 | tf_op jit(solution)/shard_map/convert_element_type | solution.py:51
  85.8 6.8 %fusion.8 = bf16[128,4,1024]{2,1,0:T(4,128)(2,1)} fusion(bf16[128,4,1024]{2,1,0:T(4,128)(2,1)S(1)} %copy-done, f32[128,4]{1,0:T(8,128)S(1)} %copy.253, f32[128,4]{1,0:T(8,128)} %copy-done.16, f32[128,4]{1,0:T(8,128)} %copy-done.15, f32[128,4]{1,0:T(8,128)S(1)} %copy-done.14, f32[128,4]{1,0:T(8,128)S(1)} %copy-done.12, f32[128,4]{1,0:T(8,128)S(1)} %copy.240, ...), kind=kLoop, calls=%fused_computation.22 | loop fusion | flops 13107200 | bytes 4767744 | tf_op jit(solution)/shard_map/convert_element_type | solution.py:58
  92.6 8.4 %all-to-all-done.1 = f32[64,1,7168]{2,1,0:T(1,128)S(1)} async-done(((f32[64,1,7168]{2,1,0:T(1,128)}), f32[64,1,7168]{2,1,0:T(1,128)S(1)}, u32[]{:S(2)}, u32[]{:S(2)}) %all-to-all-start.1) | async-done | bytes 1835040 | tf_op jit(solution)/shard_map/all_to_all | solution.py:11
  101.1 1.1 %reduce_sum.159 = f32[7168]{0:T(1024)S(1)} reduce(f32[64,1,7168]{2,1,0:T(1,128)S(1)} %all-to-all-done.1, f32[]{:T(128)} %constant.5.clone.1), dimensions={0,1}, to_apply=%region_15.0 | reduce | flops 451584 | bytes 1863684 | tf_op jit(solution)/shard_map/reduce_sum | solution.py:15
  102.2 0.6 slice_multiply_fusion.1
  102.8 0.6 div.27
  (100 shorter events, 2.9 us)
Async XLA Ops:
  0.6 6.9 %copy-start = (bf16[128,4,1024]{2,1,0:T(4,128)(2,1)S(1)}, bf16[128,4,1024]{2,1,0:T(4,128)(2,1)}, u32[]{:S(2)}) copy-start(bf16[128,4,1024]{2,1,0:T(4,128)(2,1)} %param.8) | copy-start | bytes 3145732
  0.6 6.9 %copy-start.5 = (bf16[128,4,1024]{2,1,0:T(4,128)(2,1)S(1)}, bf16[128,4,1024]{2,1,0:T(4,128)(2,1)}, u32[]{:S(2)}) copy-start(bf16[128,4,1024]{2,1,0:T(4,128)(2,1)} %param.10) | copy-start | bytes 3145732
  1.6 5.8 %copy-start.20 = (f32[1,1024]{1,0:T(1,128)}, f32[1,1024]{1,0:T(1,128)S(1)}, u32[]{:S(2)}) copy-start(f32[1,1024]{1,0:T(1,128)S(1)} %get-tuple-element.45) | copy-start | bytes 12292
  1.6 5.8 %copy-start.22 = (f32[1,1024]{1,0:T(1,128)}, f32[1,1024]{1,0:T(1,128)S(1)}, u32[]{:S(2)}) copy-start(f32[1,1024]{1,0:T(1,128)S(1)} %get-tuple-element.46) | copy-start | bytes 12292
  7.5 1.2 %copy-start.26 = (bf16[128,1024]{1,0:T(8,128)(2,1)S(1)}, bf16[128,1024]{1,0:T(8,128)(2,1)}, u32[]{:S(2)}) copy-start(bf16[128,1024]{1,0:T(8,128)(2,1)} %param.9) | copy-start | bytes 786436
  8.7 1.3 %copy-start.18 = (bf16[128,1024]{1,0:T(8,128)(2,1)S(1)}, bf16[128,1024]{1,0:T(8,128)(2,1)}, u32[]{:S(2)}) copy-start(bf16[128,1024]{1,0:T(8,128)(2,1)} %param.11) | copy-start | bytes 786436
  10.0 6.7 %copy-start.27 = (f32[3]{0:T(128)S(1)}, f32[3]{0:T(128)}, u32[]{:S(2)}) copy-start(f32[3]{0:T(128)} %param.15) | copy-start | bytes 40
  11.1 14.2 %copy-start.25 = (f32[4,6]{1,0:T(4,128)S(1)}, f32[4,6]{1,0:T(4,128)}, u32[]{:S(2)}) copy-start(f32[4,6]{1,0:T(4,128)} %param.14) | copy-start | bytes 292
  12.4 11.3 %all-to-all-start = ((f32[8,1,6656]{2,1,0:T(1,128)}), f32[8,1,6656]{2,1,0:T(1,128)S(1)}, u32[]{:S(2)}, u32[]{:S(2)}) async-start(f32[8,1,6656]{2,1,0:T(1,128)} %broadcast_in_dim.4), calls=%async_computation | async-start | bytes 425984 | tf_op jit(solution)/shard_map/all_to_all | solution.py:11
  25.3 1.2 %copy-start.17 = (f32[128,4]{1,0:T(8,128)}, f32[128,4]{1,0:T(8,128)S(1)}, u32[]{:S(2)}) copy-start(f32[128,4]{1,0:T(8,128)S(1)} %rsqrt.7) | copy-start | bytes 6148
  29.0 4.7 %copy-start.19 = (f32[6,1024]{1,0:T(8,128)S(1)}, f32[6,1024]{1,0:T(8,128)}, u32[]{:S(2)}) copy-start(f32[6,1024]{1,0:T(8,128)} %param.13) | copy-start | bytes 73732
  29.0 4.7 %copy-start.24 = (f32[1024]{0:T(1024)S(1)}, f32[1024]{0:T(1024)}, u32[]{:S(2)}) copy-start(f32[1024]{0:T(1024)} %param.12) | copy-start | bytes 12292
  29.8 6.2 %copy-start.11 = (f32[128,4]{1,0:T(8,128)}, f32[128,4]{1,0:T(8,128)S(1)}, u32[]{:S(2)}) copy-start(f32[128,4]{1,0:T(8,128)S(1)} %copy.242) | copy-start | bytes 6148
  30.0 6.0 %copy-start.13 = (f32[128,4]{1,0:T(8,128)}, f32[128,4]{1,0:T(8,128)S(1)}, u32[]{:S(2)}) copy-start(f32[128,4]{1,0:T(8,128)S(1)} %copy.244) | copy-start | bytes 6148
  30.3 5.8 %copy-start.15 = (f32[128,4]{1,0:T(8,128)}, f32[128,4]{1,0:T(8,128)S(1)}, u32[]{:S(2)}) copy-start(f32[128,4]{1,0:T(8,128)S(1)} %copy.246) | copy-start | bytes 6148
  30.5 5.5 %copy-start.16 = (f32[128,4]{1,0:T(8,128)}, f32[128,4]{1,0:T(8,128)S(1)}, u32[]{:S(2)}) copy-start(f32[128,4]{1,0:T(8,128)S(1)} %copy.248) | copy-start | bytes 6148
  36.0 65.0 %all-to-all-start.1 = ((f32[64,1,7168]{2,1,0:T(1,128)}), f32[64,1,7168]{2,1,0:T(1,128)S(1)}, u32[]{:S(2)}, u32[]{:S(2)}) async-start(f32[64,1,7168]{2,1,0:T(1,128)} %broadcast_in_dim.5), calls=%async_computation.1 | async-start | bytes 3670016 | tf_op jit(solution)/shard_map/all_to_all | solution.py:11
  58.6 0.8 copy-start.2
  58.6 2.0 %copy-start.4 = (bf16[128,1,1024]{2,1,0:T(2,128)(2,1)}, bf16[128,1,1024]{2,1,0:T(2,128)(2,1)S(1)}, u32[]{:S(2)}) copy-start(bf16[128,1,1024]{2,1,0:T(2,128)(2,1)S(1)} %get-tuple-element.26) | copy-start | bytes 786436
  58.6 2.0 %copy-start.1 = (bf16[128,1,1024]{2,1,0:T(2,128)(2,1)}, bf16[128,1,1024]{2,1,0:T(2,128)(2,1)S(1)}, u32[]{:S(2)}) copy-start(bf16[128,1,1024]{2,1,0:T(2,128)(2,1)S(1)} %get-tuple-element.23) | copy-start | bytes 786436
  58.7 2.0 %copy-start.3 = (bf16[128,1,1024]{2,1,0:T(2,128)(2,1)}, bf16[128,1,1024]{2,1,0:T(2,128)(2,1)S(1)}, u32[]{:S(2)}) copy-start(bf16[128,1,1024]{2,1,0:T(2,128)(2,1)S(1)} %get-tuple-element.25) | copy-start | bytes 786436
  80.3 5.5 %copy-start.12 = (f32[128,4]{1,0:T(8,128)S(1)}, f32[128,4]{1,0:T(8,128)}, u32[]{:S(2)}) copy-start(f32[128,4]{1,0:T(8,128)} %copy-done.11) | copy-start | bytes 6148
  80.3 5.5 %copy-start.14 = (f32[128,4]{1,0:T(8,128)S(1)}, f32[128,4]{1,0:T(8,128)}, u32[]{:S(2)}) copy-start(f32[128,4]{1,0:T(8,128)} %copy-done.13) | copy-start | bytes 6148
  80.3 5.5 %copy-start.21 = (f32[1,1024]{1,0:T(1,128)S(1)}, f32[1,1024]{1,0:T(1,128)}, u32[]{:S(2)}) copy-start(f32[1,1024]{1,0:T(1,128)} %copy-done.20) | copy-start | bytes 12292
  80.3 5.5 %copy-start.23 = (f32[1,1024]{1,0:T(1,128)S(1)}, f32[1,1024]{1,0:T(1,128)}, u32[]{:S(2)}) copy-start(f32[1,1024]{1,0:T(1,128)} %copy-done.22) | copy-start | bytes 12292
  82.0 3.8 %copy-start.6 = (f32[128,1024]{1,0:T(8,128)S(1)}, f32[128,1024]{1,0:T(8,128)}, u32[]{:S(2)}) copy-start(f32[128,1024]{1,0:T(8,128)} %convert_element_type.14) | copy-start | bytes 1572868
  82.0 3.8 %copy-start.7 = (f32[128,1024]{1,0:T(8,128)S(1)}, f32[128,1024]{1,0:T(8,128)}, u32[]{:S(2)}) copy-start(f32[128,1024]{1,0:T(8,128)} %get-tuple-element.56) | copy-start | bytes 1572868
  82.0 3.8 %copy-start.8 = (f32[128,1024]{1,0:T(8,128)S(1)}, f32[128,1024]{1,0:T(8,128)}, u32[]{:S(2)}) copy-start(f32[128,1024]{1,0:T(8,128)} %get-tuple-element.57) | copy-start | bytes 1572868
  82.0 3.8 %copy-start.9 = (f32[128,1024]{1,0:T(8,128)S(1)}, f32[128,1024]{1,0:T(8,128)}, u32[]{:S(2)}) copy-start(f32[128,1024]{1,0:T(8,128)} %get-tuple-element.58) | copy-start | bytes 1572868
  82.0 3.8 %copy-start.10 = (f32[128,1024]{1,0:T(8,128)S(1)}, f32[128,1024]{1,0:T(8,128)}, u32[]{:S(2)}) copy-start(f32[128,1024]{1,0:T(8,128)} %get-tuple-element.59) | copy-start | bytes 1572868
where the time goes:
time: 105 us; the launch traced here: 103 us
  local copies, waits for them, and re-layouts  35.9 us (34%)
  other arithmetic  27.9 us (27%)
  starting transfers between devices  20.7 us (20%)
  waiting for transfers between devices  14.2 us (14%)
  matrix products  3.45 us (3%)
  between operations  1.2 us (1%)
    all_to_all x2, starting transfers between devices, sent_to_all(): lax.all_to_all(jnp.broadcast_to(x[None], (size, *x.shape)), axis, 0, 0, t...  20.7 us
    all_to_all x2, waiting for transfers between devices, sent_to_all(): lax.all_to_all(jnp.broadcast_to(x[None], (size, *x.shape)), axis, 0, 0, t...  14.2 us
    convert_element_type x1, other arithmetic, shards(): stream_grad = total.astype(jnp.bfloat16)  6.78 us
    slice x4, local copies, waits for them, and re-layouts, shards(): coef[:, :, 2 + stream][..., None] * cotangent[:, stream, :][:, None, :]  6.57 us
    mul x4, local copies, waits for them, and re-layouts, shards(): coef[:, :, 2 + stream][..., None] * cotangent[:, stream, :][:, None, :]  5.57 us
    reduce_sum x1, other arithmetic, shards(): jnp.sum(streams * wproj[column], axis=-1)  4.79 us
    slice x1, local copies, waits for them, and re-layouts, shards(): cotangent[:, stream, :][:, None, :]  4.36 us
    slice x2, local copies, waits for them, and re-layouts, shards(): total = coef[:, :, 1][..., None] * input_cot[:, None, :]  4.14 us
  transfers between devices with their start and end apart: 2, of which 2 were waited for; matrix products, arithmetic and copies ran while one was open for 39% of the time, Pallas kernels for 0%

commit v1 on v0

v1 whole, which is shorter than its diff:
```python
import functools

import jax
import jax.numpy as jnp
from jax import lax
from jax.experimental import pallas as pl
from jax.experimental.pallas import tpu as pltpu
from jax.sharding import PartitionSpec as P

D = 8192
F32, BF16 = jnp.float32, jnp.bfloat16
NT = (((1,), (1,)), ((), ()))
NN = (((1,), (0,)), ((), ()))
TN = (((0,), (0,)), ((), ()))
GROUPS = 4
SPAN = 32
FAR_X = ((2, 0), (2, 1), (1, 0), (3, 0), (1, 1), (3, 1), (0, 1))
FAR = (4, 3, 5, 2, 6, 1, 7)
ROWS = 320


def mm(a, b, dims):
    return lax.dot_general(a, b, dims, preferred_element_type=F32)


def split(v):
    high = v.astype(BF16).astype(F32)
    return high, v - high


def body(
    h_hbm, y_hbm, g_hbm, g0_hbm, gain_hbm, proj_hbm, mix_hbm, ts_hbm,
    sg_hbm, og_hbm, pg_out, gg_out,
    h_raw, g_raw, y_s, x_s, gain_s, proj_s, mix_s, ts_s, w_s, stat, dw1, dw2, got1, got2, sg_s, og_s,
    load_sem, small_sem, out_sem, st_send, st_recv, dw_send, dw_recv,
):
    dp, tensor = lax.axis_index("dp"), lax.axis_index("tensor")
    x, core = tensor // 2, tensor % 2
    yy, zz = dp // 8, dp % 8

    smalls = [
        pltpu.make_async_copy(src, dst, small_sem.at[n])
        for n, (src, dst) in enumerate(((gain_hbm, gain_s), (proj_hbm, proj_s), (mix_hbm, mix_s), (ts_hbm, ts_s)))
    ]
    loads = []
    for i in range(GROUPS):
        part = pl.ds(i * SPAN, SPAN)
        loads.append([
            pltpu.make_async_copy(h_hbm.at[part], h_raw.at[part], load_sem.at[i, 0]),
            pltpu.make_async_copy(g_hbm.at[part], g_raw.at[part], load_sem.at[i, 1]),
            pltpu.make_async_copy(g0_hbm.at[part], x_s.at[i, pl.ds(256, SPAN)], load_sem.at[i, 2]),
            pltpu.make_async_copy(y_hbm.at[part], y_s.at[part], load_sem.at[i, 3]),
        ])
    for copy in loads[0] + smalls + loads[1] + loads[2] + loads[3]:
        copy.start()

    def tensor_peer(dx, dc):
        return {"dp": dp, "tensor": ((x + dx) % 4) * 2 + (core + dc) % 2}

    def y_peer(dy):
        return {"dp": ((yy + dy) % 8) * 8 + zz, "tensor": tensor}

    def z_peer(dz):
        return {"dp": yy * 8 + (zz + dz) % 8, "tensor": tensor}

    barrier = pltpu.get_barrier_semaphore()
    peers = [tensor_peer(*d) for d in FAR_X] + [y_peer(d) for d in FAR] + [z_peer(d) for d in FAR]
    for peer in peers:
        pl.semaphore_signal(barrier, inc=1, device_id=peer, device_id_type=pl.DeviceIdType.MESH)

    row8 = lax.broadcasted_iota(jnp.int32, (8, 128), 0)
    lane8 = lax.broadcasted_iota(jnp.int32, (8, 128), 1)
    row = lax.broadcasted_iota(jnp.int32, (128, 128), 0)
    lane = lax.broadcasted_iota(jnp.int32, (128, 128), 1)
    same = row == lane
    token = (row // 4) == (lane // 4)
    owner = row[:SPAN] == (lane[:SPAN] // 4)

    for copy in smalls:
        copy.wait()
    w_s[...] = jnp.zeros_like(w_s)
    w_s[0:6, :] = gain_s[...] * proj_s[...]
    w_hi, w_rest = split(w_s[...])
    w_mid, w_lo = split(w_rest)
    w_all = jnp.concatenate([w_hi, w_mid, w_lo, jnp.zeros_like(w_lo)], axis=0).astype(BF16)
    for i in range(GROUPS):
        x_s[i, 288:320, :] = w_all
    mixv = jnp.zeros((8, 128), F32)
    for c in range(6):
        for j in range(4):
            mixv = jnp.where((row8 == c) & (lane8 % 4 == j), mix_s[j, c], mixv)
    sv = jnp.where(row8 == 0, ts_s[0], jnp.where(row8 == 1, ts_s[1], jnp.where(row8 < 6, ts_s[2], 0.0)))

    def send_stats(i):
        copies = []
        for n, (dx, dc) in enumerate(FAR_X):
            copies.append(
                pltpu.make_async_remote_copy(
                    src_ref=stat.at[tensor, i], dst_ref=stat.at[tensor, i],
                    send_sem=st_send.at[i, n], recv_sem=st_recv.at[i, tensor],
                    device_id=tensor_peer(dx, dc), device_id_type=pl.DeviceIdType.MESH,
                )
            )
        for copy in copies:
            copy.start()
        return copies

    sends = []
    for i in range(GROUPS):
        for copy in loads[i]:
            copy.wait()
        part = pl.ds(i * SPAN, SPAN)
        x_s[i, 0:128, :] = h_raw[part].reshape(128, 1024)
        x_s[i, 128:256, :] = g_raw[part].reshape(128, 1024)
        p1 = mm(x_s[i], x_s[i, 0:128, :], NT)
        p2 = mm(y_s[part, :], x_s[i, 128:256, :], NT)
        square = jnp.sum(jnp.where(same, p1[0:128], 0.0), axis=0, keepdims=True)
        dmix = jnp.sum(jnp.where(token, p1[128:256], 0.0).reshape(16, 8, 128), axis=0)
        dmix = dmix + pltpu.roll(dmix, 4, 0)
        dalpha = jnp.sum(jnp.where(owner, p1[256:288], 0.0), axis=0, keepdims=True)
        dbeta = jnp.sum(jnp.where(owner, p2, 0.0), axis=0, keepdims=True)
        lin = p1[288:296] + p1[296:304] + p1[304:312]
        stat[tensor, i, 0:8, :] = jnp.where(row8 == 6, square, lin)
        stat[tensor, i, 8:16, :] = jnp.where(
            row8 == 0, dbeta, jnp.where(row8 == 1, dalpha, jnp.where(row8 < 6, pltpu.roll(dmix, 2, 0), 0.0))
        )
        if i == 0:
            pl.semaphore_wait(barrier, len(peers))
        sends += send_stats(i)

    coefs, dlins, dsq2s = [], [], []
    dw = jnp.zeros((8, 1024), F32)
    for i in range(GROUPS):
        for dx, dc in FAR_X:
            other = ((x + dx) % 4) * 2 + (core + dc) % 2
            pltpu.make_async_remote_copy(
                src_ref=stat.at[other, i], dst_ref=stat.at[other, i],
                send_sem=st_send.at[i, 0], recv_sem=st_recv.at[i, other],
                device_id=tensor_peer(dx, dc), device_id_type=pl.DeviceIdType.MESH,
            ).wait_recv()
        total = stat[0, i]
        for n in range(1, 8):
            total = total + stat[n, i]
        lin, dcoef = total[0:8], total[8:16]
        inv = lax.rsqrt(total[6:7] / D + 1e-06)
        bent = jnp.tanh(inv * lin)
        dpre = dcoef * sv * (1.0 - bent * bent)
        dlin = dpre * inv
        coefs.append(mixv + sv * bent)
        dlins.append(dlin)
        dsq2s.append(-1.0 * (inv * inv * inv) / D * jnp.sum(dpre * lin, axis=0, keepdims=True))
        d_hi, d_rest = split(dlin)
        d_mid, d_lo = split(d_rest)
        left = jnp.concatenate([d_hi, d_mid, d_lo, jnp.zeros_like(d_lo)], axis=0).astype(BF16)
        part = mm(left, x_s[i, 0:128, :], NN)
        dw = dw + (part[0:8] + part[8:16] + part[16:24])

    for q in range(8):
        a, b = q // 4, q % 4
        dw1[a, 6 * b : 6 * b + 6, :] = dw[0:6, 128 * q : 128 * q + 128]

    def exchange(step, source, got, along):
        own = (yy, zz)
        copies = []
        for n, far in enumerate(FAR):
            for a in range(2):
                axis = along[a]
                copies.append(
                    pltpu.make_async_remote_copy(
                        src_ref=source.at[a], dst_ref=got.at[a, own[axis]],
                        send_sem=dw_send.at[step, a, n], recv_sem=dw_recv.at[step, a, own[axis]],
                        device_id=(y_peer, z_peer)[axis](far), device_id_type=pl.DeviceIdType.MESH,
                    )
                )
        for copy in copies:
            copy.start()
        for a in range(2):
            got[a, own[along[a]]] = source[a]
        return copies

    def arrive(step, source, got, along):
        own = (yy, zz)
        for far in FAR:
            for a in range(2):
                other = (own[along[a]] + far) % 8
                pltpu.make_async_remote_copy(
                    src_ref=source.at[a], dst_ref=got.at[a, other],
                    send_sem=dw_send.at[step, a, 0], recv_sem=dw_recv.at[step, a, other],
                    device_id=(y_peer, z_peer)[along[a]](far), device_id_type=pl.DeviceIdType.MESH,
                ).wait_recv()
        sums = []
        for a in range(2):
            total = got[a, 0]
            for n in range(1, 8):
                total = total + got[a, n]
            sums.append(total)
        return sums

    def grads(i):
        coef, dlin, dsq2 = coefs[i], dlins[i], dsq2s[i]
        mix8 = jnp.where(row8 < 4, pltpu.roll(coef, 6, 0), pltpu.roll(coef, 2, 0))
        mixer = jnp.where(token, jnp.broadcast_to(mix8[None], (16, 8, 128)).reshape(128, 128), 0.0)
        diag = jnp.where(same, dsq2, 0.0)
        alpha = jnp.where(owner, coef[1:2], 0.0)
        left = jnp.concatenate([diag, mixer, alpha, dlin, dlin, dlin, jnp.zeros_like(dlin)], axis=0)
        high, low = split(left)
        both = jnp.concatenate([high.T, low.T], axis=0).astype(BF16)
        beta = jnp.where(owner, coef[0:1], 0.0)
        b_high, b_low = split(beta)
        b_both = jnp.concatenate([b_high, b_low], axis=0).astype(BF16)
        part = pl.ds(i * SPAN, SPAN)
        for n in range(4):
            columns = slice(256 * n, 256 * n + 256)
            out = mm(both, x_s[i, :, columns], NN)
            sg_s[part, :, columns] = (out[0:128] + out[128:256]).astype(BF16).reshape(SPAN, 4, 256)
            out = mm(b_both, x_s[i, 128:256, columns], NN)
            og_s[part, columns] = (out[0:SPAN] + out[SPAN : 2 * SPAN]).astype(BF16)
        copies = [
            pltpu.make_async_copy(sg_s.at[part], sg_hbm.at[part], out_sem.at[i, 0]),
            pltpu.make_async_copy(og_s.at[part], og_hbm.at[part], out_sem.at[i, 1]),
        ]
        for copy in copies:
            copy.start()
        return copies

    sends += exchange(0, dw1, got1, (0, 1))
    stores = grads(0) + grads(1)
    for a, total in enumerate(arrive(0, dw1, got1, (0, 1))):
        dw2[a] = total
    sends += exchange(1, dw2, got2, (1, 0))
    stores += grads(2) + grads(3)
    sums = arrive(1, dw2, got2, (1, 0))
    per_proj = 1.0 / (4.0 * 64 * 128 * D) ** 0.5
    per_gain = 1.0 / (4.0 * 64 * 128) ** 0.5
    for q in range(8):
        a, b = q // 4, q % 4
        columns = slice(128 * q, 128 * q + 128)
        total = sums[a][6 * b : 6 * b + 6]
        pg_out[:, columns] = gain_s[:, columns] * total * per_proj
        gg_out[:, columns] = jnp.sum(total * proj_s[:, columns], axis=0, keepdims=True) * per_gain
    for copy in stores:
        copy.wait()
    for copy in sends:
        copy.wait_send()


def shards(streams, layer_out, cotangent, input_cot, gain, projection, static_mix, tanh_scale):
    anywhere = pl.BlockSpec(memory_space=pl.ANY)
    vmem = pl.BlockSpec(memory_space=pltpu.VMEM)
    sg, og, pg, gg = pl.pallas_call(
        body,
        out_shape=(
            jax.ShapeDtypeStruct(streams.shape, BF16),
            jax.ShapeDtypeStruct(layer_out.shape, BF16),
            jax.ShapeDtypeStruct((6, 1024), F32),
            jax.ShapeDtypeStruct((1, 1024), F32),
        ),
        in_specs=[anywhere] * 8,
        out_specs=(anywhere, anywhere, vmem, vmem),
        scratch_shapes=[
            pltpu.VMEM((128, 4, 1024), BF16),
            pltpu.VMEM((128, 4, 1024), BF16),
            pltpu.VMEM((128, 1024), BF16),
            pltpu.VMEM((GROUPS, ROWS, 1024), BF16),
            pltpu.VMEM((1, 1024), F32),
            pltpu.VMEM((6, 1024), F32),
            pltpu.SMEM((4, 6), F32),
            pltpu.SMEM((3,), F32),
            pltpu.VMEM((8, 1024), F32),
            pltpu.VMEM((8, GROUPS, 16, 128), F32),
            pltpu.VMEM((2, 24, 128), F32),
            pltpu.VMEM((2, 24, 128), F32),
            pltpu.VMEM((2, 8, 24, 128), F32),
            pltpu.VMEM((2, 8, 24, 128), F32),
            pltpu.VMEM((128, 4, 1024), BF16),
            pltpu.VMEM((128, 1024), BF16),
            pltpu.SemaphoreType.DMA((GROUPS, 4)),
            pltpu.SemaphoreType.DMA((4,)),
            pltpu.SemaphoreType.DMA((GROUPS, 2)),
            pltpu.SemaphoreType.DMA((GROUPS, 7)),
            pltpu.SemaphoreType.DMA((GROUPS, 8)),
            pltpu.SemaphoreType.DMA((2, 2, 7)),
            pltpu.SemaphoreType.DMA((2, 2, 8)),
        ],
        compiler_params=pltpu.CompilerParams(collective_id=0, has_side_effects=True),
    )(streams, layer_out, cotangent, input_cot, gain.reshape(1, 1024), projection, static_mix, tanh_scale)
    return sg, og, pg, gg.reshape(1024)


def solution(mesh):
    placed = (
        P("dp", None, "tensor"),
        P("dp", "tensor"),
        P("dp", None, "tensor"),
        P("dp", "tensor"),
        P("tensor"),
        P(None, "tensor"),
        P(),
        P(),
    )
    return jax.shard_map(
        shards,
        mesh=mesh,
        in_specs=placed,
        out_specs=(P("dp", None, "tensor"), P("dp", "tensor"), P(None, "tensor"), P("tensor")),
        check_vma=False,
    )
```

time: 105 us -> 37.4 us (0.36)
  the two profiles are of different devices: /device:TPU:24 before, /device:TPU:1 now
where the time goes in v1:
time: 37.4 us; the launch traced here: 37.2 us
  Pallas kernels  31.9 us (85%)
  local copies, waits for them, and re-layouts  4.63 us (12%)
  between operations  0.65 us (2%)
    pallas_call x1, Pallas kernels, shards(): pl.pallas_call(body, out_shape=(jax.ShapeDtypeStruct(streams.shape, BF16)...  31.9 us
    unnamed x10, local copies, waits for them, and re-layouts  4.63 us

profile of v1, /device:TPU:1, one launch (start us, length us, event | category | flops | bytes accessed | tf_op | source)
XLA Modules:
  0.0 37.2 jit_solution(10964538568793196987)
XLA Ops:
  0.6 31.9 %shard_map.111 = (bf16[128,4,1024]{2,1,0:T(4,128)(2,1)}, bf16[128,1024]{1,0:T(8,128)(2,1)}, f32[6,1024]{1,0:T(8,128)}, f32[1,1024]{1,0:T(1,128)}) custom-call(bf16[128,4,1024]{2,1,0:T(4,128)(2,1)} %h_hbm.1, bf16[128,1024]{1,0:T(8,128)(2,1)} %y_hbm.1, bf16[128,4,1024]{2,1,0:T(4,128)(2,1)} %g_hbm.1, bf16[128,1024]{1,0:T(8,128)(2,1)} %g0_hbm.1, ...), custom_call_target="tpu_custom_call" | custom-call | tf_op jit(solution)/shard_map/pallas_call | solution.py:250
  32.5 0.0 copy-start
  32.5 2.6 %copy.16 = bf16[128,4,1024]{2,1,0:T(4,128)(2,1)} copy(bf16[128,4,1024]{2,1,0:T(4,128)(2,1)} %get-tuple-element.16) | data formatting | bytes 2097152
  35.1 0.0 copy-done
  35.1 0.0 copy-start.1
  35.1 0.7 %copy.17 = bf16[128,1024]{1,0:T(8,128)(2,1)} copy(bf16[128,1024]{1,0:T(8,128)(2,1)S(1)} %copy-done) | data formatting | bytes 524288
  35.8 0.1 copy-done.1
  35.9 0.0 copy-start.2
  35.9 0.6 %copy.18 = f32[6,1024]{1,0:T(8,128)} copy(f32[6,1024]{1,0:T(8,128)S(1)} %copy-done.1) | data formatting | bytes 49152
  36.5 0.1 copy-done.2
  36.6 0.6 %copy.19 = f32[1024]{0:T(1024)} copy(f32[1024]{0:T(1024)S(1)} %bitcast.3) | data formatting | bytes 8192
Async XLA Ops:
  32.5 2.6 %copy-start = (bf16[128,1024]{1,0:T(8,128)(2,1)S(1)}, bf16[128,1024]{1,0:T(8,128)(2,1)}, u32[]{:S(2)}) copy-start(bf16[128,1024]{1,0:T(8,128)(2,1)} %get-tuple-element.17) | copy-start | bytes 786436
  35.1 0.8 %copy-start.1 = (f32[6,1024]{1,0:T(8,128)S(1)}, f32[6,1024]{1,0:T(8,128)}, u32[]{:S(2)}) copy-start(f32[6,1024]{1,0:T(8,128)} %get-tuple-element.18) | copy-start | bytes 73732
  35.9 0.7 %copy-start.2 = (f32[1,1024]{1,0:T(1,128)S(1)}, f32[1,1024]{1,0:T(1,128)}, u32[]{:S(2)}) copy-start(f32[1,1024]{1,0:T(1,128)} %get-tuple-element.11) | copy-start | bytes 12292

commit v2 on v1

--- a/solution.py
+++ b/solution.py
@@ -30,9 +30,9 @@
 
 def body(
     h_hbm, y_hbm, g_hbm, g0_hbm, gain_hbm, proj_hbm, mix_hbm, ts_hbm,
-    sg_hbm, og_hbm, pg_out, gg_out,
-    h_raw, g_raw, y_s, x_s, gain_s, proj_s, mix_s, ts_s, w_s, stat, dw1, dw2, got1, got2, sg_s, og_s,
-    load_sem, small_sem, out_sem, st_send, st_recv, dw_send, dw_recv,
+    sg_s, og_s, pg_out, gg_out,
+    h_raw, g_raw, y_s, x_s, gain_s, proj_s, mix_s, ts_s, w_s, own_s, near_s, stat, dw1, dw2, got1, got2,
+    load_sem, small_sem, near_send, near_recv, st_send, st_recv, dw_send, dw_recv,
 ):
     dp, tensor = lax.axis_index("dp"), lax.axis_index("tensor")
     x, core = tensor // 2, tensor % 2
@@ -43,13 +43,14 @@
         for n, (src, dst) in enumerate(((gain_hbm, gain_s), (proj_hbm, proj_s), (mix_hbm, mix_s), (ts_hbm, ts_s)))
     ]
     loads = []
-    for i in range(GROUPS):
-        part = pl.ds(i * SPAN, SPAN)
+    order = (1 - core, 3 - core, core, 2 + core)
+    for k, g in enumerate(order):
+        part = pl.ds(pl.multiple_of(g * SPAN, SPAN), SPAN)
         loads.append([
-            pltpu.make_async_copy(h_hbm.at[part], h_raw.at[part], load_sem.at[i, 0]),
-            pltpu.make_async_copy(g_hbm.at[part], g_raw.at[part], load_sem.at[i, 1]),
-            pltpu.make_async_copy(g0_hbm.at[part], x_s.at[i, pl.ds(256, SPAN)], load_sem.at[i, 2]),
-            pltpu.make_async_copy(y_hbm.at[part], y_s.at[part], load_sem.at[i, 3]),
+            pltpu.make_async_copy(h_hbm.at[part], h_raw.at[part], load_sem.at[k, 0]),
+            pltpu.make_async_copy(g_hbm.at[part], g_raw.at[part], load_sem.at[k, 1]),
+            pltpu.make_async_copy(g0_hbm.at[part], x_s.at[g, pl.ds(256, SPAN)], load_sem.at[k, 2]),
+            pltpu.make_async_copy(y_hbm.at[part], y_s.at[g], load_sem.at[k, 3]),
         ])
     for copy in loads[0] + smalls + loads[1] + loads[2] + loads[3]:
         copy.start()
@@ -91,69 +92,85 @@
             mixv = jnp.where((row8 == c) & (lane8 % 4 == j), mix_s[j, c], mixv)
     sv = jnp.where(row8 == 0, ts_s[0], jnp.where(row8 == 1, ts_s[1], jnp.where(row8 < 6, ts_s[2], 0.0)))
 
-    def send_stats(i):
-        copies = []
-        for n, (dx, dc) in enumerate(FAR_X):
-            copies.append(
-                pltpu.make_async_remote_copy(
-                    src_ref=stat.at[tensor, i], dst_ref=stat.at[tensor, i],
-                    send_sem=st_send.at[i, n], recv_sem=st_recv.at[i, tensor],
-                    device_id=tensor_peer(dx, dc), device_id_type=pl.DeviceIdType.MESH,
-                )
-            )
-        for copy in copies:
-            copy.start()
-        return copies
-
-    sends = []
-    for i in range(GROUPS):
-        for copy in loads[i]:
+    def inner(g, k):
+        for copy in loads[k]:
             copy.wait()
-        part = pl.ds(i * SPAN, SPAN)
-        x_s[i, 0:128, :] = h_raw[part].reshape(128, 1024)
-        x_s[i, 128:256, :] = g_raw[part].reshape(128, 1024)
-        p1 = mm(x_s[i], x_s[i, 0:128, :], NT)
-        p2 = mm(y_s[part, :], x_s[i, 128:256, :], NT)
+        x_s[g, 0:128, :] = h_raw[pl.ds(g * SPAN, SPAN)].reshape(128, 1024)
+        x_s[g, 128:256, :] = g_raw[pl.ds(g * SPAN, SPAN)].reshape(128, 1024)
+        p1 = mm(x_s[g], x_s[g, 0:128, :], NT)
+        p2 = mm(y_s[g], x_s[g, 128:256, :], NT)
         square = jnp.sum(jnp.where(same, p1[0:128], 0.0), axis=0, keepdims=True)
         dmix = jnp.sum(jnp.where(token, p1[128:256], 0.0).reshape(16, 8, 128), axis=0)
         dmix = dmix + pltpu.roll(dmix, 4, 0)
         dalpha = jnp.sum(jnp.where(owner, p1[256:288], 0.0), axis=0, keepdims=True)
         dbeta = jnp.sum(jnp.where(owner, p2, 0.0), axis=0, keepdims=True)
         lin = p1[288:296] + p1[296:304] + p1[304:312]
-        stat[tensor, i, 0:8, :] = jnp.where(row8 == 6, square, lin)
-        stat[tensor, i, 8:16, :] = jnp.where(
+        own_s[g, 0:8, :] = jnp.where(row8 == 6, square, lin)
+        own_s[g, 8:16, :] = jnp.where(
             row8 == 0, dbeta, jnp.where(row8 == 1, dalpha, jnp.where(row8 < 6, pltpu.roll(dmix, 2, 0), 0.0))
         )
-        if i == 0:
+
+    def pass_on(k):
+        g = order[k]
+        return pltpu.make_async_remote_copy(
+            src_ref=own_s.at[g], dst_ref=near_s.at[k],
+            send_sem=near_send.at[k], recv_sem=near_recv.at[k],
+            device_id=tensor_peer(0, 1), device_id_type=pl.DeviceIdType.MESH,
+        )
+
+    sends = []
+    for k in range(GROUPS):
+        inner(order[k], k)
+        if k == 0:
             pl.semaphore_wait(barrier, len(peers))
-        sends += send_stats(i)
+        if k < 2:
+            copy = pass_on(k)
+            copy.start()
+            sends.append(copy)
+    for k in range(2):
+        g = order[2 + k]
+        pass_on(k).wait_recv()
+        stat[x, g] = own_s[g] + near_s[k]
+        copies = [
+            pltpu.make_async_remote_copy(
+                src_ref=stat.at[x, g], dst_ref=stat.at[x, g],
+                send_sem=st_send.at[k, n], recv_sem=st_recv.at[x, g],
+                device_id=tensor_peer(dx, dc), device_id_type=pl.DeviceIdType.MESH,
+            )
+            for n, (dx, dc) in enumerate(FAR_X)
+        ]
+        for copy in copies:
+            copy.start()
+        sends += copies
+
+    def stats_in(chip, g):
+        pltpu.make_async_remote_copy(
+            src_ref=stat.at[chip, g], dst_ref=stat.at[chip, g],
+            send_sem=st_send.at[0, 0], recv_sem=st_recv.at[chip, g],
+            device_id=tensor_peer(0, 1), device_id_type=pl.DeviceIdType.MESH,
+        ).wait_recv()
 
     coefs, dlins, dsq2s = [], [], []
     dw = jnp.zeros((8, 1024), F32)
-    for i in range(GROUPS):
-        for dx, dc in FAR_X:
-            other = ((x + dx) % 4) * 2 + (core + dc) % 2
-            pltpu.make_async_remote_copy(
-                src_ref=stat.at[other, i], dst_ref=stat.at[other, i],
-                send_sem=st_send.at[i, 0], recv_sem=st_recv.at[i, other],
-                device_id=tensor_peer(dx, dc), device_id_type=pl.DeviceIdType.MESH,
-            ).wait_recv()
-        total = stat[0, i]
-        for n in range(1, 8):
-            total = total + stat[n, i]
-        lin, dcoef = total[0:8], total[8:16]
-        inv = lax.rsqrt(total[6:7] / D + 1e-06)
-        bent = jnp.tanh(inv * lin)
-        dpre = dcoef * sv * (1.0 - bent * bent)
-        dlin = dpre * inv
-        coefs.append(mixv + sv * bent)
-        dlins.append(dlin)
-        dsq2s.append(-1.0 * (inv * inv * inv) / D * jnp.sum(dpre * lin, axis=0, keepdims=True))
-        d_hi, d_rest = split(dlin)
-        d_mid, d_lo = split(d_rest)
-        left = jnp.concatenate([d_hi, d_mid, d_lo, jnp.zeros_like(d_lo)], axis=0).astype(BF16)
-        part = mm(left, x_s[i, 0:128, :], NN)
-        dw = dw + (part[0:8] + part[8:16] + part[16:24])
+    for k in range(2):
+        stats_in(x, order[k])
+        for dx in (1, 3, 2):
+            for n in range(2):
+                stats_in((x + dx) % 4, 2 * k + n)
+        for i in (2 * k, 2 * k + 1):
+            total = (stat[0, i] + stat[1, i]) + (stat[2, i] + stat[3, i])
+            lin, dcoef = total[0:8], total[8:16]
+            inv = lax.rsqrt(total[6:7] / D + 1e-06)
+            bent = jnp.tanh(inv * lin)
+            dpre = dcoef * sv * (1.0 - bent * bent)
+            dlin = dpre * inv
+            coefs.append(mixv + sv * bent)
+            dlins.append(dlin)
+            dsq2s.append(-1.0 * (inv * inv * inv) / D * jnp.sum(dpre * lin, axis=0, keepdims=True))
+            d_hi, d_lo = split(dlin)
+            left = jnp.concatenate([d_hi, d_lo], axis=0).astype(BF16)
+            part = mm(left, x_s[i, 0:128, :], NN)
+            dw = dw + (part[0:8] + part[8:16])
 
     for q in range(8):
         a, b = q // 4, q % 4
@@ -215,20 +232,15 @@
             sg_s[part, :, columns] = (out[0:128] + out[128:256]).astype(BF16).reshape(SPAN, 4, 256)
             out = mm(b_both, x_s[i, 128:256, columns], NN)
             og_s[part, columns] = (out[0:SPAN] + out[SPAN : 2 * SPAN]).astype(BF16)
-        copies = [
-            pltpu.make_async_copy(sg_s.at[part], sg_hbm.at[part], out_sem.at[i, 0]),
-            pltpu.make_async_copy(og_s.at[part], og_hbm.at[part], out_sem.at[i, 1]),
-        ]
-        for copy in copies:
-            copy.start()
-        return copies
 
     sends += exchange(0, dw1, got1, (0, 1))
-    stores = grads(0) + grads(1)
+    grads(0)
+    grads(1)
     for a, total in enumerate(arrive(0, dw1, got1, (0, 1))):
         dw2[a] = total
     sends += exchange(1, dw2, got2, (1, 0))
-    stores += grads(2) + grads(3)
+    grads(2)
+    grads(3)
     sums = arrive(1, dw2, got2, (1, 0))
     per_proj = 1.0 / (4.0 * 64 * 128 * D) ** 0.5
     per_gain = 1.0 / (4.0 * 64 * 128) ** 0.5
@@ -238,10 +250,16 @@
         total = sums[a][6 * b : 6 * b + 6]
         pg_out[:, columns] = gain_s[:, columns] * total * per_proj
         gg_out[:, columns] = jnp.sum(total * proj_s[:, columns], axis=0, keepdims=True) * per_gain
-    for copy in stores:
-        copy.wait()
     for copy in sends:
         copy.wait_send()
+
+
+def store(*refs):
+    copies = [pltpu.make_async_copy(refs[n], refs[4 + n], refs[8].at[n]) for n in range(4)]
+    for copy in copies:
+        copy.start()
+    for copy in copies:
+        copy.wait()
 
 
 def shards(streams, layer_out, cotangent, input_cot, gain, projection, static_mix, tanh_scale):
@@ -250,40 +268,49 @@
     sg, og, pg, gg = pl.pallas_call(
         body,
         out_shape=(
-            jax.ShapeDtypeStruct(streams.shape, BF16),
-            jax.ShapeDtypeStruct(layer_out.shape, BF16),
-            jax.ShapeDtypeStruct((6, 1024), F32),
-            jax.ShapeDtypeStruct((1, 1024), F32),
+            pltpu.VMEM(streams.shape, BF16),
+            pltpu.VMEM(layer_out.shape, BF16),
+            pltpu.VMEM((6, 1024), F32),
+            pltpu.VMEM((1, 1024), F32),
         ),
         in_specs=[anywhere] * 8,
-        out_specs=(anywhere, anywhere, vmem, vmem),
+        out_specs=(vmem,) * 4,
         scratch_shapes=[
             pltpu.VMEM((128, 4, 1024), BF16),
             pltpu.VMEM((128, 4, 1024), BF16),
-            pltpu.VMEM((128, 1024), BF16),
+            pltpu.VMEM((GROUPS, SPAN, 1024), BF16),
             pltpu.VMEM((GROUPS, ROWS, 1024), BF16),
             pltpu.VMEM((1, 1024), F32),
             pltpu.VMEM((6, 1024), F32),
             pltpu.SMEM((4, 6), F32),
             pltpu.SMEM((3,), F32),
             pltpu.VMEM((8, 1024), F32),
-            pltpu.VMEM((8, GROUPS, 16, 128), F32),
+            pltpu.VMEM((GROUPS, 16, 128), F32),
+            pltpu.VMEM((2, 16, 128), F32),
+            pltpu.VMEM((4, GROUPS, 16, 128), F32),
             pltpu.VMEM((2, 24, 128), F32),
             pltpu.VMEM((2, 24, 128), F32),
             pltpu.VMEM((2, 8, 24, 128), F32),
             pltpu.VMEM((2, 8, 24, 128), F32),
-            pltpu.VMEM((128, 4, 1024), BF16),
-            pltpu.VMEM((128, 1024), BF16),
             pltpu.SemaphoreType.DMA((GROUPS, 4)),
             pltpu.SemaphoreType.DMA((4,)),
-            pltpu.SemaphoreType.DMA((GROUPS, 2)),
-            pltpu.SemaphoreType.DMA((GROUPS, 7)),
-            pltpu.SemaphoreType.DMA((GROUPS, 8)),
+            pltpu.SemaphoreType.DMA((2,)),
+            pltpu.SemaphoreType.DMA((2,)),
+            pltpu.SemaphoreType.DMA((2, 7)),
+            pltpu.SemaphoreType.DMA((4, GROUPS)),
             pltpu.SemaphoreType.DMA((2, 2, 7)),
             pltpu.SemaphoreType.DMA((2, 2, 8)),
         ],
         compiler_params=pltpu.CompilerParams(collective_id=0, has_side_effects=True),
     )(streams, layer_out, cotangent, input_cot, gain.reshape(1, 1024), projection, static_mix, tanh_scale)
+    made = (sg, og, pg, gg)
+    sg, og, pg, gg = pl.pallas_call(
+        store,
+        out_shape=tuple(jax.ShapeDtypeStruct(a.shape, a.dtype) for a in made),
+        in_specs=[vmem] * 4,
+        out_specs=(anywhere,) * 4,
+        scratch_shapes=[pltpu.SemaphoreType.DMA((4,))],
+    )(*(pltpu.with_memory_space_constraint(a, pltpu.VMEM) for a in made))
     return sg, og, pg, gg.reshape(1024)
 
 

time: 37.4 us -> 33 us (0.88)
  local copies, waits for them, and re-layouts: 4.63 us -> 0 us
    unnamed x10 -> x0, local copies, waits for them, and re-layouts: 4.63 us -> none
    pallas_call x1 -> x2, Pallas kernels: 31.9 us -> 32.2 us  [the longest x1 31.1 us: shards(): pl.pallas_call(body, out_shape=(pltpu.VMEM(streams.shape, BF16), pltpu.VM...]
where the time goes in v2:
time: 33 us; the launch traced here: 32.9 us
  Pallas kernels  32.2 us (98%)
  between operations  0.64 us (2%)
    pallas_call x1, Pallas kernels, shards(): pl.pallas_call(body, out_shape=(pltpu.VMEM(streams.shape, BF16), pltpu.VM...  31.1 us
    pallas_call x1, Pallas kernels, shards(): pl.pallas_call(store, out_shape=tuple((jax.ShapeDtypeStruct(a.shape, a.dt...  1.09 us

profile of v2, /device:TPU:1, one launch (start us, length us, event | category | flops | bytes accessed | tf_op | source)
XLA Modules:
  0.0 32.9 jit_solution(496685518003227636)
XLA Ops:
  0.6 31.1 %shard_map.111 = (bf16[128,4,1024]{2,1,0:T(4,128)(2,1)S(1)}, bf16[128,1024]{1,0:T(8,128)(2,1)S(1)}, f32[6,1024]{1,0:T(8,128)S(1)}, f32[1,1024]{1,0:T(1,128)S(1)}) custom-call(bf16[128,4,1024]{2,1,0:T(4,128)(2,1)} %h_hbm.1, bf16[128,1024]{1,0:T(8,128)(2,1)} %y_hbm.1, bf16[128,4,1024]{2,1,0:T(4,128)(2,1)} %g_hbm.1, bf16[128,1024]{1,0:T(8,128)(2,1)} %g0_hbm.1, ...), custom_call_target="tpu_custom_call" | custom-call | tf_op jit(solution)/shard_map/pallas_call | solution.py:268
  31.8 1.1 %shard_map.112 = (bf16[128,4,1024]{2,1,0:T(4,128)(2,1)}, bf16[128,1024]{1,0:T(8,128)(2,1)}, f32[6,1024]{1,0:T(8,128)}, f32[1,1024]{1,0:T(1,128)}) custom-call(bf16[128,4,1024]{2,1,0:T(4,128)(2,1)S(1)} %get-tuple-element.12.refs_0_, bf16[128,1024]{1,0:T(8,128)(2,1)S(1)} %get-tuple-element.13.refs_1_, f32[6,1024]{1,0:T(8,128)S(1)} %get-tuple-element.14.refs_2_, ...), custom_call_target="tpu_custom_call" | custom-call | tf_op jit(solution)/shard_map/pallas_call | solution.py:307

commit v3 on v2

v3 whole, which is shorter than its diff:
```python
import functools

import jax
import jax.numpy as jnp
from jax import lax
from jax.experimental import pallas as pl
from jax.experimental.pallas import tpu as pltpu
from jax.sharding import PartitionSpec as P

D = 8192
F32, BF16 = jnp.float32, jnp.bfloat16
NT = (((1,), (1,)), ((), ()))
NN = (((1,), (0,)), ((), ()))
TN = (((0,), (0,)), ((), ()))
GROUPS = 4
SPAN = 32
FAR_X = ((2, 0), (2, 1), (1, 0), (3, 0), (1, 1), (3, 1), (0, 1))
ROWS = 320


def mm(a, b, dims):
    return lax.dot_general(a, b, dims, preferred_element_type=F32)


def split(v):
    high = v.astype(BF16).astype(F32)
    return high, v - high


def body(
    h_hbm, y_hbm, g_hbm, g0_hbm, gain_hbm, proj_hbm, mix_hbm, ts_hbm,
    sg_s, og_s, pg_out, gg_out,
    h_raw, g_raw, y_s, x_s, gain_s, proj_s, mix_s, ts_s, w_s, own_s, near_s, stat, coef_s, dw1, dw2, got1, got2,
    load_sem, small_sem, near_recv, st_send, st_recv, dw_send, dw_recv,
):
    dp, tensor = lax.axis_index("dp"), lax.axis_index("tensor")
    x, core = tensor // 2, tensor % 2
    yy, zz = dp // 8, dp % 8

    order = (1 - core, 3 - core, core, 2 + core)

    def loads(k):
        part = pl.ds(pl.multiple_of(order[k] * SPAN, SPAN), SPAN)
        for src, dst in (
            (h_hbm.at[part], h_raw.at[part]),
            (g_hbm.at[part], g_raw.at[part]),
            (g0_hbm.at[part], x_s.at[order[k], pl.ds(256, SPAN)]),
            (y_hbm.at[part], y_s.at[order[k]]),
        ):
            pltpu.make_async_copy(src, dst, load_sem.at[k]).start()

    smalls = [
        pltpu.make_async_copy(src, dst, small_sem.at[n])
        for n, (src, dst) in enumerate(((mix_hbm, mix_s), (ts_hbm, ts_s), (gain_hbm, gain_s), (proj_hbm, proj_s)))
    ]
    for copy in smalls:
        copy.start()
    loads(0)

    def arrived(like, sem):
        pltpu.make_async_copy(like, like, sem).wait()

    def tensor_peer(dx, dc):
        return {"dp": dp, "tensor": ((x + dx) % 4) * 2 + (core + dc) % 2}

    def y_peer(n):
        return {"dp": (n + (n + 8 - yy) // 8) * 8 + zz, "tensor": tensor}

    def z_peer(n):
        return {"dp": yy * 8 + n + (n + 8 - zz) // 8, "tensor": tensor}

    barrier = pltpu.get_barrier_semaphore()
    peers = [peer(n) for n in range(7) for peer in (y_peer, z_peer)] + [tensor_peer(*d) for d in FAR_X]
    for peer in peers:
        pl.semaphore_signal(barrier, inc=1, device_id=peer, device_id_type=pl.DeviceIdType.MESH)
    for k in range(1, GROUPS):
        loads(k)

    row8 = lax.broadcasted_iota(jnp.int32, (8, 128), 0)
    lane8 = lax.broadcasted_iota(jnp.int32, (8, 128), 1)
    row = lax.broadcasted_iota(jnp.int32, (128, 128), 0)
    lane = lax.broadcasted_iota(jnp.int32, (128, 128), 1)
    same = row == lane
    token = (row // 4) == (lane // 4)
    owner = row[:SPAN] == (lane[:SPAN] // 4)

    for copy in smalls:
        copy.wait()
    w_s[...] = jnp.zeros_like(w_s)
    w_s[0:6, :] = gain_s[...] * proj_s[...]
    w_hi, w_rest = split(w_s[...])
    w_mid, w_lo = split(w_rest)
    w_all = jnp.concatenate([w_hi, w_mid, w_lo, jnp.zeros_like(w_lo)], axis=0).astype(BF16)
    for i in range(GROUPS):
        x_s[i, 288:320, :] = w_all
    mixv = jnp.zeros((8, 128), F32)
    for c in range(6):
        for j in range(4):
            mixv = jnp.where((row8 == c) & (lane8 % 4 == j), mix_s[j, c], mixv)
    sv = jnp.where(row8 == 0, ts_s[0], jnp.where(row8 == 1, ts_s[1], jnp.where(row8 < 6, ts_s[2], 0.0)))

    def inner(g, k):
        arrived(x_s.at[g], load_sem.at[k])
        x_s[g, 0:128, :] = h_raw[pl.ds(g * SPAN, SPAN)].reshape(128, 1024)
        x_s[g, 128:256, :] = g_raw[pl.ds(g * SPAN, SPAN)].reshape(128, 1024)
        left, right = slice(0, 512), slice(512, 1024)
        p1 = mm(x_s[g, :, left], x_s[g, 0:128, left], NT) + mm(x_s[g, :, right], x_s[g, 0:128, right], NT)
        p2 = mm(y_s[g, :, left], x_s[g, 128:256, left], NT) + mm(y_s[g, :, right], x_s[g, 128:256, right], NT)
        square = jnp.sum(jnp.where(same, p1[0:128], 0.0), axis=0, keepdims=True)
        dmix = jnp.sum(jnp.where(token, p1[128:256], 0.0).reshape(16, 8, 128), axis=0)
        dmix = dmix + pltpu.roll(dmix, 4, 0)
        dalpha = jnp.sum(jnp.where(owner, p1[256:288], 0.0), axis=0, keepdims=True)
        dbeta = jnp.sum(jnp.where(owner, p2, 0.0), axis=0, keepdims=True)
        lin = p1[288:296] + p1[296:304] + p1[304:312]
        own_s[g, 0:8, :] = jnp.where(row8 == 6, square, jnp.where(row8 == 7, dbeta, lin))
        own_s[g, 8:13, :] = jnp.where(row8 == 0, dalpha, pltpu.roll(dmix, 1, 0))[0:5]

    def pass_on(k):
        return pltpu.make_async_remote_copy(
            src_ref=own_s.at[order[k]], dst_ref=near_s.at[k],
            send_sem=st_send, recv_sem=near_recv.at[k],
            device_id=tensor_peer(0, 1), device_id_type=pl.DeviceIdType.MESH,
        )

    inner(order[0], 0)
    inner(order[1], 1)
    inner(order[2], 2)
    pl.semaphore_wait(barrier, len(peers))
    pass_on(0).start()
    pass_on(1).start()
    inner(order[3], 3)
    for k in range(2):
        slot = x * GROUPS + order[2 + k]
        pass_on(k).wait_recv()
        stat[slot] = own_s[order[2 + k]] + near_s[k]
        for dx, dc in FAR_X:
            pltpu.make_async_remote_copy(
                src_ref=stat.at[slot], dst_ref=stat.at[slot],
                send_sem=st_send, recv_sem=st_recv.at[k],
                device_id=tensor_peer(dx, dc), device_id_type=pl.DeviceIdType.MESH,
            ).start()

    dw = jnp.zeros((8, 1024), F32)
    for k in range(2):
        arrived(stat.at[pl.ds(0, 7)], st_recv.at[k])
        for i in (2 * k, 2 * k + 1):
            total = (stat[i] + stat[4 + i]) + (stat[8 + i] + stat[12 + i])
            lin = total[0:8]
            dcoef = jnp.concatenate([total[7:13], jnp.zeros((2, 128), F32)], axis=0)
            inv = lax.rsqrt(total[6:7] / D + 1e-06)
            bent = jnp.tanh(inv * lin)
            dpre = dcoef * sv * (1.0 - bent * bent)
            dlin = dpre * inv
            coef_s[i, 0:8, :] = mixv + sv * bent
            coef_s[i, 8:16, :] = dlin
            dsq2 = -1.0 * (inv * inv * inv) / D * jnp.sum(dpre * lin, axis=0, keepdims=True)
            coef_s[i, 16:24, :] = jnp.broadcast_to(dsq2, (8, 128))
            d_hi, d_lo = split(dlin)
            left = jnp.concatenate([d_hi, d_lo], axis=0).astype(BF16)
            part = mm(left, x_s[i, 0:128, :], NN)
            dw = dw + (part[0:8] + part[8:16])

    for q in range(8):
        a, b = q // 4, q % 4
        dw1[a, 6 * b : 6 * b + 6, :] = dw[0:6, 128 * q : 128 * q + 128]

    def give(step, a, source, got, axis):
        own = (yy, zz)[axis]
        for n in range(7):
            pltpu.make_async_remote_copy(
                src_ref=source.at[a], dst_ref=got.at[a, own],
                send_sem=dw_send.at[step], recv_sem=dw_recv.at[step, a],
                device_id=(y_peer, z_peer)[axis](n), device_id_type=pl.DeviceIdType.MESH,
            ).start()
        got[a, own] = source[a]

    def take(step, a, got):
        arrived(got.at[a, pl.ds(0, 7)], dw_recv.at[step, a])
        total = got[a, 0]
        for n in range(1, 8):
            total = total + got[a, n]
        return total

    def grads(i, carry):
        coef, dlin, dsq2 = coef_s[i, 0:8, :], coef_s[i, 8:16, :], coef_s[i, 16:17, :]
        mix8 = jnp.where(row8 < 4, pltpu.roll(coef, 6, 0), pltpu.roll(coef, 2, 0))
        mixer = jnp.where(token, jnp.broadcast_to(mix8[None], (16, 8, 128)).reshape(128, 128), 0.0)
        diag = jnp.where(same, dsq2, 0.0)
        alpha = jnp.where(owner, coef[1:2], 0.0)
        left = jnp.concatenate([diag, mixer, alpha, dlin, dlin, dlin, jnp.zeros_like(dlin)], axis=0)
        high, low = split(left)
        both = jnp.concatenate([high.T, low.T], axis=0).astype(BF16)
        beta = jnp.where(owner, coef[0:1], 0.0)
        b_high, b_low = split(beta)
        b_both = jnp.concatenate([b_high, b_low], axis=0).astype(BF16)
        part = pl.ds(pl.multiple_of(i * SPAN, SPAN), SPAN)
        for n in range(4):
            columns = slice(256 * n, 256 * n + 256)
            out = mm(both, x_s[i, :, columns], NN)
            sg_s[part, :, columns] = (out[0:128] + out[128:256]).astype(BF16).reshape(SPAN, 4, 256)
            out = mm(b_both, x_s[i, 128:256, columns], NN)
            og_s[part, columns] = (out[0:SPAN] + out[SPAN : 2 * SPAN]).astype(BF16)
        return carry

    give(0, 0, dw1, got1, 0)
    give(0, 1, dw1, got1, 1)
    lax.fori_loop(0, 2, grads, 0)
    for a in range(2):
        dw2[a] = take(0, a, got1)
        give(1, a, dw2, got2, 1 - a)
    lax.fori_loop(2, 4, grads, 0)
    sums = [take(1, 0, got2), take(1, 1, got2)]
    per_proj = 1.0 / (4.0 * 64 * 128 * D) ** 0.5
    per_gain = 1.0 / (4.0 * 64 * 128) ** 0.5
    for q in range(8):
        a, b = q // 4, q % 4
        columns = slice(128 * q, 128 * q + 128)
        total = sums[a][6 * b : 6 * b + 6]
        pg_out[:, columns] = gain_s[:, columns] * total * per_proj
        gg_out[:, columns] = jnp.sum(total * proj_s[:, columns], axis=0, keepdims=True) * per_gain
    arrived(stat, st_send)
    arrived(got1.at[:, pl.ds(0, 7)], dw_send.at[0])
    arrived(got2.at[:, pl.ds(0, 7)], dw_send.at[1])


def store(*refs):
    copies = [pltpu.make_async_copy(refs[n], refs[4 + n], refs[8].at[n]) for n in range(4)]
    for copy in copies:
        copy.start()
    for copy in copies:
        copy.wait()


def shards(streams, layer_out, cotangent, input_cot, gain, projection, static_mix, tanh_scale):
    anywhere = pl.BlockSpec(memory_space=pl.ANY)
    vmem = pl.BlockSpec(memory_space=pltpu.VMEM)
    sg, og, pg, gg = pl.pallas_call(
        body,
        out_shape=(
            pltpu.VMEM(streams.shape, BF16),
            pltpu.VMEM(layer_out.shape, BF16),
            pltpu.VMEM((6, 1024), F32),
            pltpu.VMEM((1, 1024), F32),
        ),
        in_specs=[anywhere] * 8,
        out_specs=(vmem,) * 4,
        scratch_shapes=[
            pltpu.VMEM((128, 4, 1024), BF16),
            pltpu.VMEM((128, 4, 1024), BF16),
            pltpu.VMEM((GROUPS, SPAN, 1024), BF16),
            pltpu.VMEM((GROUPS, ROWS, 1024), BF16),
            pltpu.VMEM((1, 1024), F32),
            pltpu.VMEM((6, 1024), F32),
            pltpu.SMEM((4, 6), F32),
            pltpu.SMEM((3,), F32),
            pltpu.VMEM((8, 1024), F32),
            pltpu.VMEM((GROUPS, 13, 128), F32),
            pltpu.VMEM((2, 13, 128), F32),
            pltpu.VMEM((4 * GROUPS, 13, 128), F32),
            pltpu.VMEM((GROUPS, 24, 128), F32),
            pltpu.VMEM((2, 24, 128), F32),
            pltpu.VMEM((2, 24, 128), F32),
            pltpu.VMEM((2, 8, 24, 128), F32),
            pltpu.VMEM((2, 8, 24, 128), F32),
            pltpu.SemaphoreType.DMA((GROUPS,)),
            pltpu.SemaphoreType.DMA((4,)),
            pltpu.SemaphoreType.DMA((2,)),
            pltpu.SemaphoreType.DMA,
            pltpu.SemaphoreType.DMA((2,)),
            pltpu.SemaphoreType.DMA((2,)),
            pltpu.SemaphoreType.DMA((2, 2)),
        ],
        compiler_params=pltpu.CompilerParams(collective_id=0, has_side_effects=True),
    )(streams, layer_out, cotangent, input_cot, gain.reshape(1, 1024), projection, static_mix, tanh_scale)
    made = (sg, og, pg, gg)
    sg, og, pg, gg = pl.pallas_call(
        store,
        out_shape=tuple(jax.ShapeDtypeStruct(a.shape, a.dtype) for a in made),
        in_specs=[vmem] * 4,
        out_specs=(anywhere,) * 4,
        scratch_shapes=[pltpu.SemaphoreType.DMA((4,))],
    )(*(pltpu.with_memory_space_constraint(a, pltpu.VMEM) for a in made))
    return sg, og, pg, gg.reshape(1024)


def solution(mesh):
    placed = (
        P("dp", None, "tensor"),
        P("dp", "tensor"),
        P("dp", None, "tensor"),
        P("dp", "tensor"),
        P("tensor"),
        P(None, "tensor"),
        P(),
        P(),
    )
    return jax.shard_map(
        shards,
        mesh=mesh,
        in_specs=placed,
        out_specs=(P("dp", None, "tensor"), P("dp", "tensor"), P(None, "tensor"), P("tensor")),
        check_vma=False,
    )
```

time: 33 us -> 30.4 us (0.921)
  Pallas kernels: 32.2 us -> 29.5 us
    pallas_call x1, Pallas kernels: 31.1 us -> 28.4 us  [shards(): pl.pallas_call(body, out_shape=(pltpu.VMEM(streams.shape, BF16), pltpu.VM...]
where the time goes in v3:
time: 30.4 us; the launch traced here: 30.1 us
  Pallas kernels  29.5 us (97%)
  between operations  0.64 us (2%)
    pallas_call x1, Pallas kernels, shards(): pl.pallas_call(body, out_shape=(pltpu.VMEM(streams.shape, BF16), pltpu.VM...  28.4 us
    pallas_call x1, Pallas kernels, shards(): pl.pallas_call(store, out_shape=tuple((jax.ShapeDtypeStruct(a.shape, a.dt...  1.09 us

profile of v3, /device:TPU:1, one launch (start us, length us, event | category | flops | bytes accessed | tf_op | source)
XLA Modules:
  0.0 30.1 jit_solution(9543525526334523622)
XLA Ops:
  0.6 28.4 %shard_map.111 = (bf16[128,4,1024]{2,1,0:T(4,128)(2,1)S(1)}, bf16[128,1024]{1,0:T(8,128)(2,1)S(1)}, f32[6,1024]{1,0:T(8,128)S(1)}, f32[1,1024]{1,0:T(1,128)S(1)}) custom-call(bf16[128,4,1024]{2,1,0:T(4,128)(2,1)} %h_hbm.1, bf16[128,1024]{1,0:T(8,128)(2,1)} %y_hbm.1, bf16[128,4,1024]{2,1,0:T(4,128)(2,1)} %g_hbm.1, bf16[128,1024]{1,0:T(8,128)(2,1)} %g0_hbm.1, ...), custom_call_target="tpu_custom_call" | custom-call | tf_op jit(solution)/shard_map/pallas_call | solution.py:237
  29.0 1.1 %shard_map.112 = (bf16[128,4,1024]{2,1,0:T(4,128)(2,1)}, bf16[128,1024]{1,0:T(8,128)(2,1)}, f32[6,1024]{1,0:T(8,128)}, f32[1,1024]{1,0:T(1,128)}) custom-call(bf16[128,4,1024]{2,1,0:T(4,128)(2,1)S(1)} %get-tuple-element.12.refs_0_, bf16[128,1024]{1,0:T(8,128)(2,1)S(1)} %get-tuple-element.13.refs_1_, f32[6,1024]{1,0:T(8,128)S(1)} %get-tuple-element.14.refs_2_, ...), custom_call_target="tpu_custom_call" | custom-call | tf_op jit(solution)/shard_map/pallas_call | solution.py:276

commit v4 on v3

--- a/solution.py
+++ b/solution.py
@@ -32,6 +32,7 @@
     sg_s, og_s, pg_out, gg_out,
     h_raw, g_raw, y_s, x_s, gain_s, proj_s, mix_s, ts_s, w_s, own_s, near_s, stat, coef_s, dw1, dw2, got1, got2,
     load_sem, small_sem, near_recv, st_send, st_recv, dw_send, dw_recv,
+    beside, across, all_in,
 ):
     dp, tensor = lax.axis_index("dp"), lax.axis_index("tensor")
     x, core = tensor // 2, tensor % 2
@@ -70,9 +71,21 @@
         return {"dp": yy * 8 + n + (n + 8 - zz) // 8, "tensor": tensor}
 
     barrier = pltpu.get_barrier_semaphore()
-    peers = [peer(n) for n in range(7) for peer in (y_peer, z_peer)] + [tensor_peer(*d) for d in FAR_X]
-    for peer in peers:
-        pl.semaphore_signal(barrier, inc=1, device_id=peer, device_id_type=pl.DeviceIdType.MESH)
+    role = (tensor + 6) % 8
+
+    def signal(sem, peer):
+        pl.semaphore_signal(sem, inc=1, device_id=peer, device_id_type=pl.DeviceIdType.MESH)
+
+    def at(n):
+        return {"dp": dp, "tensor": (n + 2) % 8}
+
+    for n in range(6):
+        signal(barrier, at(n + (n + 7 - role) // 7))
+
+    @pl.when(role == 7)
+    def _():
+        signal(barrier, at(6))
+
     for k in range(1, GROUPS):
         loads(k)
 
@@ -123,13 +136,22 @@
         )
 
     inner(order[0], 0)
-    inner(order[1], 1)
-    inner(order[2], 2)
-    pl.semaphore_wait(barrier, len(peers))
-    pass_on(0).start()
-    pass_on(1).start()
-    inner(order[3], 3)
-    for k in range(2):
+    @pl.when(role < 7)
+    def _():
+        pl.semaphore_wait(barrier, 7)
+
+    @pl.when(role == 6)
+    def _():
+        signal(beside, at(7))
+        for n in range(7):
+            for peer in (y_peer, z_peer):
+                signal(barrier, {"dp": peer(n)["dp"], "tensor": 1})
+
+    @pl.when(role < 6)
+    def _():
+        signal(across, at(7))
+
+    def tell(k):
         slot = x * GROUPS + order[2 + k]
         pass_on(k).wait_recv()
         stat[slot] = own_s[order[2 + k]] + near_s[k]
@@ -139,6 +161,29 @@
                 send_sem=st_send, recv_sem=st_recv.at[k],
                 device_id=tensor_peer(dx, dc), device_id_type=pl.DeviceIdType.MESH,
             ).start()
+
+    @pl.when(role == 7)
+    def _():
+        pl.semaphore_wait(beside, 1)
+
+    pass_on(0).start()
+    inner(order[1], 1)
+    pass_on(1).start()
+    inner(order[2], 2)
+
+    @pl.when(role == 7)
+    def _():
+        pl.semaphore_wait(across, 6)
+
+    tell(0)
+    inner(order[3], 3)
+    tell(1)
+
+    @pl.when(role == 7)
+    def _():
+        pl.semaphore_wait(barrier, 14)
+        for n in range(7):
+            signal(all_in, at(n))
 
     dw = jnp.zeros((8, 1024), F32)
     for k in range(2):
@@ -201,6 +246,11 @@
             out = mm(b_both, x_s[i, 128:256, columns], NN)
             og_s[part, columns] = (out[0:SPAN] + out[SPAN : 2 * SPAN]).astype(BF16)
         return carry
+
+
+    @pl.when(role < 7)
+    def _():
+        pl.semaphore_wait(all_in, 1)
 
     give(0, 0, dw1, got1, 0)
     give(0, 1, dw1, got1, 1)
@@ -269,6 +319,9 @@
             pltpu.SemaphoreType.DMA((2,)),
             pltpu.SemaphoreType.DMA((2,)),
             pltpu.SemaphoreType.DMA((2, 2)),
+            pltpu.SemaphoreType.REGULAR,
+            pltpu.SemaphoreType.REGULAR,
+            pltpu.SemaphoreType.REGULAR,
         ],
         compiler_params=pltpu.CompilerParams(collective_id=0, has_side_effects=True),
     )(streams, layer_out, cotangent, input_cot, gain.reshape(1, 1024), projection, static_mix, tanh_scale)

time: 30.4 us -> 29.7 us (0.977)
  Pallas kernels: 29.5 us -> 28.5 us
    pallas_call x1, Pallas kernels: 28.4 us -> 27.4 us  [shards(): pl.pallas_call(body, out_shape=(pltpu.VMEM(streams.shape, BF16), pltpu.VM...]
where the time goes in v4:
time: 29.7 us; the launch traced here: 29.2 us
  Pallas kernels  28.5 us (96%)
  between operations  0.64 us (2%)
    pallas_call x1, Pallas kernels, shards(): pl.pallas_call(body, out_shape=(pltpu.VMEM(streams.shape, BF16), pltpu.VM...  27.4 us
    pallas_call x1, Pallas kernels, shards(): pl.pallas_call(store, out_shape=tuple((jax.ShapeDtypeStruct(a.shape, a.dt...  1.09 us

profile of v4, /device:TPU:1, one launch (start us, length us, event | category | flops | bytes accessed | tf_op | source)
XLA Modules:
  0.0 29.2 jit_solution(1281500225681164260)
XLA Ops:
  0.6 27.4 %shard_map.111 = (bf16[128,4,1024]{2,1,0:T(4,128)(2,1)S(1)}, bf16[128,1024]{1,0:T(8,128)(2,1)S(1)}, f32[6,1024]{1,0:T(8,128)S(1)}, f32[1,1024]{1,0:T(1,128)S(1)}) custom-call(bf16[128,4,1024]{2,1,0:T(4,128)(2,1)} %h_hbm.1, bf16[128,1024]{1,0:T(8,128)(2,1)} %y_hbm.1, bf16[128,4,1024]{2,1,0:T(4,128)(2,1)} %g_hbm.1, bf16[128,1024]{1,0:T(8,128)(2,1)} %g0_hbm.1, ...), custom_call_target="tpu_custom_call" | custom-call | tf_op jit(solution)/shard_map/pallas_call | solution.py:287
  28.1 1.1 %shard_map.112 = (bf16[128,4,1024]{2,1,0:T(4,128)(2,1)}, bf16[128,1024]{1,0:T(8,128)(2,1)}, f32[6,1024]{1,0:T(8,128)}, f32[1,1024]{1,0:T(1,128)}) custom-call(bf16[128,4,1024]{2,1,0:T(4,128)(2,1)S(1)} %get-tuple-element.12.refs_0_, bf16[128,1024]{1,0:T(8,128)(2,1)S(1)} %get-tuple-element.13.refs_1_, f32[6,1024]{1,0:T(8,128)S(1)} %get-tuple-element.14.refs_2_, ...), custom_call_target="tpu_custom_call" | custom-call | tf_op jit(solution)/shard_map/pallas_call | solution.py:329

commit v5 on v4

--- a/solution.py
+++ b/solution.py
@@ -43,10 +43,10 @@
     def loads(k):
         part = pl.ds(pl.multiple_of(order[k] * SPAN, SPAN), SPAN)
         for src, dst in (
-            (h_hbm.at[part], h_raw.at[part]),
-            (g_hbm.at[part], g_raw.at[part]),
-            (g0_hbm.at[part], x_s.at[order[k], pl.ds(256, SPAN)]),
-            (y_hbm.at[part], y_s.at[order[k]]),
+            (h_hbm.at[part], h_raw.at[k]),
+            (g_hbm.at[part], g_raw.at[k]),
+            (g0_hbm.at[part], x_s.at[k, pl.ds(256, SPAN)]),
+            (y_hbm.at[part], y_s.at[k]),
         ):
             pltpu.make_async_copy(src, dst, load_sem.at[k]).start()
 
@@ -112,30 +112,35 @@
             mixv = jnp.where((row8 == c) & (lane8 % 4 == j), mix_s[j, c], mixv)
     sv = jnp.where(row8 == 0, ts_s[0], jnp.where(row8 == 1, ts_s[1], jnp.where(row8 < 6, ts_s[2], 0.0)))
 
-    def inner(g, k):
-        arrived(x_s.at[g], load_sem.at[k])
-        x_s[g, 0:128, :] = h_raw[pl.ds(g * SPAN, SPAN)].reshape(128, 1024)
-        x_s[g, 128:256, :] = g_raw[pl.ds(g * SPAN, SPAN)].reshape(128, 1024)
-        left, right = slice(0, 512), slice(512, 1024)
-        p1 = mm(x_s[g, :, left], x_s[g, 0:128, left], NT) + mm(x_s[g, :, right], x_s[g, 0:128, right], NT)
-        p2 = mm(y_s[g, :, left], x_s[g, 128:256, left], NT) + mm(y_s[g, :, right], x_s[g, 128:256, right], NT)
+    def inner(k):
+        x_s[k, 0:128, :] = h_raw[k].reshape(128, 1024)
+        x_s[k, 128:256, :] = g_raw[k].reshape(128, 1024)
+        p1 = mm(x_s[k], x_s[k, 0:128, :], NT)
+        p2 = mm(y_s[k], x_s[k, 128:256, :], NT)
         square = jnp.sum(jnp.where(same, p1[0:128], 0.0), axis=0, keepdims=True)
         dmix = jnp.sum(jnp.where(token, p1[128:256], 0.0).reshape(16, 8, 128), axis=0)
         dmix = dmix + pltpu.roll(dmix, 4, 0)
         dalpha = jnp.sum(jnp.where(owner, p1[256:288], 0.0), axis=0, keepdims=True)
         dbeta = jnp.sum(jnp.where(owner, p2, 0.0), axis=0, keepdims=True)
         lin = p1[288:296] + p1[296:304] + p1[304:312]
-        own_s[g, 0:8, :] = jnp.where(row8 == 6, square, jnp.where(row8 == 7, dbeta, lin))
-        own_s[g, 8:13, :] = jnp.where(row8 == 0, dalpha, pltpu.roll(dmix, 1, 0))[0:5]
+        own_s[k, 0:8, :] = jnp.where(row8 == 6, square, jnp.where(row8 == 7, dbeta, lin))
+        own_s[k, 8:13, :] = jnp.where(row8 == 0, dalpha, pltpu.roll(dmix, 1, 0))[0:5]
 
     def pass_on(k):
         return pltpu.make_async_remote_copy(
-            src_ref=own_s.at[order[k]], dst_ref=near_s.at[k],
+            src_ref=own_s.at[k], dst_ref=near_s.at[k],
             send_sem=st_send, recv_sem=near_recv.at[k],
             device_id=tensor_peer(0, 1), device_id_type=pl.DeviceIdType.MESH,
         )
 
-    inner(order[0], 0)
+    def pair(k):
+        for n in (k, k + 1):
+            arrived(x_s.at[n], load_sem.at[n])
+        inner(k)
+        inner(k + 1)
+
+    pair(0)
+
     @pl.when(role < 7)
     def _():
         pl.semaphore_wait(barrier, 7)
@@ -154,7 +159,7 @@
     def tell(k):
         slot = x * GROUPS + order[2 + k]
         pass_on(k).wait_recv()
-        stat[slot] = own_s[order[2 + k]] + near_s[k]
+        stat[slot] = own_s[2 + k] + near_s[k]
         for dx, dc in FAR_X:
             pltpu.make_async_remote_copy(
                 src_ref=stat.at[slot], dst_ref=stat.at[slot],
@@ -162,21 +167,21 @@
                 device_id=tensor_peer(dx, dc), device_id_type=pl.DeviceIdType.MESH,
             ).start()
 
+    @pl.when(role < 7)
+    def _():
+        pass_on(0).start()
+        pass_on(1).start()
+
+    pair(2)
+
     @pl.when(role == 7)
     def _():
         pl.semaphore_wait(beside, 1)
-
-    pass_on(0).start()
-    inner(order[1], 1)
-    pass_on(1).start()
-    inner(order[2], 2)
-
-    @pl.when(role == 7)
-    def _():
+        pass_on(0).start()
+        pass_on(1).start()
         pl.semaphore_wait(across, 6)
 
     tell(0)
-    inner(order[3], 3)
     tell(1)
 
     @pl.when(role == 7)
@@ -188,8 +193,9 @@
     dw = jnp.zeros((8, 1024), F32)
     for k in range(2):
         arrived(stat.at[pl.ds(0, 7)], st_recv.at[k])
-        for i in (2 * k, 2 * k + 1):
-            total = (stat[i] + stat[4 + i]) + (stat[8 + i] + stat[12 + i])
+        for i in (k, k + 2):
+            g = order[i]
+            total = (stat[g] + stat[4 + g]) + (stat[8 + g] + stat[12 + g])
             lin = total[0:8]
             dcoef = jnp.concatenate([total[7:13], jnp.zeros((2, 128), F32)], axis=0)
             inv = lax.rsqrt(total[6:7] / D + 1e-06)
@@ -238,7 +244,8 @@
         beta = jnp.where(owner, coef[0:1], 0.0)
         b_high, b_low = split(beta)
         b_both = jnp.concatenate([b_high, b_low], axis=0).astype(BF16)
-        part = pl.ds(pl.multiple_of(i * SPAN, SPAN), SPAN)
+        g = 2 * (i % 2) + (i // 2) * core + (1 - i // 2) * (1 - core)
+        part = pl.ds(pl.multiple_of(g * SPAN, SPAN), SPAN)
         for n in range(4):
             columns = slice(256 * n, 256 * n + 256)
             out = mm(both, x_s[i, :, columns], NN)
@@ -295,8 +302,8 @@
         in_specs=[anywhere] * 8,
         out_specs=(vmem,) * 4,
         scratch_shapes=[
-            pltpu.VMEM((128, 4, 1024), BF16),
-            pltpu.VMEM((128, 4, 1024), BF16),
+            pltpu.VMEM((GROUPS, SPAN, 4, 1024), BF16),
+            pltpu.VMEM((GROUPS, SPAN, 4, 1024), BF16),
             pltpu.VMEM((GROUPS, SPAN, 1024), BF16),
             pltpu.VMEM((GROUPS, ROWS, 1024), BF16),
             pltpu.VMEM((1, 1024), F32),

time: 29.7 us -> 29.7 us (level)
  no operation moved by 1% of the time
where the time goes in v5:
time: 29.7 us; the launch traced here: 29.2 us
  Pallas kernels  28.6 us (96%)
  between operations  0.64 us (2%)
    pallas_call x1, Pallas kernels, shards(): pl.pallas_call(body, out_shape=(pltpu.VMEM(streams.shape, BF16), pltpu.VM...  27.5 us
    pallas_call x1, Pallas kernels, shards(): pl.pallas_call(store, out_shape=tuple((jax.ShapeDtypeStruct(a.shape, a.dt...  1.09 us

profile of v5, /device:TPU:1, one launch (start us, length us, event | category | flops | bytes accessed | tf_op | source)
XLA Modules:
  0.0 29.2 jit_solution(5954725171306391742)
XLA Ops:
  0.6 27.5 %shard_map.111 = (bf16[128,4,1024]{2,1,0:T(4,128)(2,1)S(1)}, bf16[128,1024]{1,0:T(8,128)(2,1)S(1)}, f32[6,1024]{1,0:T(8,128)S(1)}, f32[1,1024]{1,0:T(1,128)S(1)}) custom-call(bf16[128,4,1024]{2,1,0:T(4,128)(2,1)} %h_hbm.1, bf16[128,1024]{1,0:T(8,128)(2,1)} %y_hbm.1, bf16[128,4,1024]{2,1,0:T(4,128)(2,1)} %g_hbm.1, bf16[128,1024]{1,0:T(8,128)(2,1)} %g0_hbm.1, ...), custom_call_target="tpu_custom_call" | custom-call | tf_op jit(solution)/shard_map/pallas_call | solution.py:294
  28.1 1.1 %shard_map.112 = (bf16[128,4,1024]{2,1,0:T(4,128)(2,1)}, bf16[128,1024]{1,0:T(8,128)(2,1)}, f32[6,1024]{1,0:T(8,128)}, f32[1,1024]{1,0:T(1,128)}) custom-call(bf16[128,4,1024]{2,1,0:T(4,128)(2,1)S(1)} %get-tuple-element.12.refs_0_, bf16[128,1024]{1,0:T(8,128)(2,1)S(1)} %get-tuple-element.13.refs_1_, f32[6,1024]{1,0:T(8,128)S(1)} %get-tuple-element.14.refs_2_, ...), custom_call_target="tpu_custom_call" | custom-call | tf_op jit(solution)/shard_map/pallas_call | solution.py:336

commit v6 on v5

--- a/solution.py
+++ b/solution.py
@@ -48,7 +48,7 @@
             (g0_hbm.at[part], x_s.at[k, pl.ds(256, SPAN)]),
             (y_hbm.at[part], y_s.at[k]),
         ):
-            pltpu.make_async_copy(src, dst, load_sem.at[k]).start()
+            pltpu.make_async_copy(src, dst, load_sem.at[k // 2]).start()
 
     smalls = [
         pltpu.make_async_copy(src, dst, small_sem.at[n])
@@ -134,8 +134,7 @@
         )
 
     def pair(k):
-        for n in (k, k + 1):
-            arrived(x_s.at[n], load_sem.at[n])
+        arrived(x_s.at[pl.ds(k, 2)], load_sem.at[k // 2])
         inner(k)
         inner(k + 1)
 
@@ -319,7 +318,7 @@
             pltpu.VMEM((2, 24, 128), F32),
             pltpu.VMEM((2, 8, 24, 128), F32),
             pltpu.VMEM((2, 8, 24, 128), F32),
-            pltpu.SemaphoreType.DMA((GROUPS,)),
+            pltpu.SemaphoreType.DMA((2,)),
             pltpu.SemaphoreType.DMA((4,)),
             pltpu.SemaphoreType.DMA((2,)),
             pltpu.SemaphoreType.DMA,

time: 29.7 us -> 29.7 us (level)
  no operation moved by 1% of the time
where the time goes in v6:
time: 29.7 us; the launch traced here: 29.2 us
  Pallas kernels  28.5 us (96%)
  between operations  0.64 us (2%)
    pallas_call x1, Pallas kernels, shards(): pl.pallas_call(body, out_shape=(pltpu.VMEM(streams.shape, BF16), pltpu.VM...  27.4 us
    pallas_call x1, Pallas kernels, shards(): pl.pallas_call(store, out_shape=tuple((jax.ShapeDtypeStruct(a.shape, a.dt...  1.09 us

profile of v6, /device:TPU:1, one launch (start us, length us, event | category | flops | bytes accessed | tf_op | source)
XLA Modules:
  0.0 29.2 jit_solution(17785048298556102546)
XLA Ops:
  0.6 27.4 %shard_map.111 = (bf16[128,4,1024]{2,1,0:T(4,128)(2,1)S(1)}, bf16[128,1024]{1,0:T(8,128)(2,1)S(1)}, f32[6,1024]{1,0:T(8,128)S(1)}, f32[1,1024]{1,0:T(1,128)S(1)}) custom-call(bf16[128,4,1024]{2,1,0:T(4,128)(2,1)} %h_hbm.1, bf16[128,1024]{1,0:T(8,128)(2,1)} %y_hbm.1, bf16[128,4,1024]{2,1,0:T(4,128)(2,1)} %g_hbm.1, bf16[128,1024]{1,0:T(8,128)(2,1)} %g0_hbm.1, ...), custom_call_target="tpu_custom_call" | custom-call | tf_op jit(solution)/shard_map/pallas_call | solution.py:293
  28.1 1.1 %shard_map.112 = (bf16[128,4,1024]{2,1,0:T(4,128)(2,1)}, bf16[128,1024]{1,0:T(8,128)(2,1)}, f32[6,1024]{1,0:T(8,128)}, f32[1,1024]{1,0:T(1,128)}) custom-call(bf16[128,4,1024]{2,1,0:T(4,128)(2,1)S(1)} %get-tuple-element.12.refs_0_, bf16[128,1024]{1,0:T(8,128)(2,1)S(1)} %get-tuple-element.13.refs_1_, f32[6,1024]{1,0:T(8,128)S(1)} %get-tuple-element.14.refs_2_, ...), custom_call_target="tpu_custom_call" | custom-call | tf_op jit(solution)/shard_map/pallas_call | solution.py:335
